TPU v7x, 128 devices: a whole 4x4x4 slice. The times are simulated.
128 devices in a mesh: section: 8 (over x, y_lo), dp: 16 (over z, y_hi, core).
Axes of the slice: x: 4, y: 4 (y_hi: 2, y_lo: 2; y = y_hi * 2 + y_lo), z: 4, core: 2. Of those that a mesh axis runs over, the one named last changes fastest.
Arguments:
- inputs: bfloat16 [32, 128, 3072], P('dp'), may hold values from -6 to 6
- sample_ids: int32 [16, 2], P('dp'), may hold values from 0 to 1, each once within a row
- stored: bfloat16 [8, 2, 32, 128, 3072], P('section', None, 'dp'), may hold values from -4 to 4, as said below
- weight: bfloat16 [8, 3072, 3072], P('section'), may hold values from -0.109375 to 0.109375
- norm_gain: float32 [8, 3072], P('section'), may hold values from 0.1 to 1.9
Outputs:
- section_outputs: bfloat16 [8, 32, 128, 3072], P('section', 'dp')
- weight_grads: bfloat16 [8, 3072, 3072], P('section', 'dp')
Inputs may be any that keep to these rules, and one draw needn't show every extreme that they name: `sample_ids`: each row names each of the replica's 2 samples once. `stored`: copy 0 of section s equals copy 1 of section s - 1, and copy 0 of section 0 equals copy 1 of the last section.
All inputs are finite; a program needn't handle non-finite values.
Results may differ from a plain program's by a relative error of at most 0.024.
Values may be sent and summed in bfloat16 or wider, within the bound.
A program may use at most 192 MiB of HBM per device.

v0:
```python
from functools import partial
import math

import jax
import jax.numpy as jnp
from jax import lax
from jax.sharding import PartitionSpec as P

epsilon = 1e-05
delta_bound = 2.0


def from_behind(shard, axis, by):
    length = lax.axis_size(axis)
    pairs = [(i, i + by) for i in range(length) if 0 <= i + by < length]
    return lax.ppermute(shard, axis, pairs)


def activate(values):
    return jax.nn.gelu(values, approximate=False)


def normalize(state, norm_gain):
    average = jnp.mean(state, axis=-1, keepdims=True)
    centred = state - average
    variance = jnp.mean(centred * centred, axis=-1, keepdims=True)
    return centred * lax.rsqrt(variance + epsilon) * norm_gain


def forward_layer(state, layer_gain, layer_weight):
    normed = normalize(state, layer_gain).astype(jnp.bfloat16)
    preact = jnp.dot(normed, layer_weight, preferred_element_type=jnp.float32)
    return (normed, preact)


def pick(table, index):
    return lax.dynamic_index_in_dim(table, index, 0, keepdims=False)


def place(table, value, index):
    return lax.dynamic_update_index_in_dim(table, value, index, 0)


def per_device(inputs, sample_ids, stored, weight, norm_gain):
    num_sections = lax.axis_size("section")
    section_pos = lax.axis_index("section")
    num_batches, tokens, width = inputs.shape
    rows_total = num_batches * tokens
    layer_weight = weight[0]
    layer_gain = norm_gain[0]
    own_ids = sample_ids[0]
    recv_store = stored[0, 0]
    send_store = stored[0, 1]
    steps_total = num_batches + num_sections - 1
    is_first = section_pos == 0
    is_last = section_pos == num_sections - 1
    loss_scale = 1.0 / math.sqrt(lax.axis_size("dp") * rows_total)
    zero_act = jnp.zeros((tokens, width), jnp.bfloat16)
    stash_init = {
        "states": jnp.zeros((num_batches, tokens, width), jnp.float32),
        "results": jnp.zeros((num_batches, tokens, width), jnp.bfloat16),
    }
    stash_init["normed"] = jnp.zeros((num_batches, tokens, width), jnp.bfloat16)
    stash_init["preact"] = jnp.zeros((num_batches, tokens, width), jnp.float32)

    def forward_step(step, carry):
        incoming, stash = carry
        batch = step - section_pos
        valid = jnp.logical_and(batch >= 0, batch < num_batches)
        slot = jnp.clip(batch, 0, num_batches - 1)
        sample = pick(own_ids, slot)

        def forward_compute(stash_now):
            given = pick(inputs, slot).astype(jnp.float32)
            rebuilt = pick(recv_store, sample).astype(jnp.float32) + incoming.astype(jnp.float32)
            state = jnp.where(is_first, given, rebuilt)
            normed, preact = forward_layer(state, layer_gain, layer_weight)
            result = state + activate(preact)
            reference_copy = pick(send_store, sample).astype(jnp.float32)
            clipped = jnp.clip(result - reference_copy, -delta_bound, delta_bound).astype(
                jnp.bfloat16
            )
            updated = dict(stash_now)
            updated["states"] = place(stash_now["states"], state, slot)
            updated["results"] = place(stash_now["results"], result.astype(jnp.bfloat16), slot)
            updated["normed"] = place(stash_now["normed"], normed, slot)
            updated["preact"] = place(stash_now["preact"], preact, slot)
            return (clipped, updated)

        def forward_skip(stash_now):
            return (zero_act, stash_now)

        clipped, stash = lax.cond(valid, forward_compute, forward_skip, stash)
        outgoing = from_behind(clipped, "section", 1)
        return (outgoing, stash)

    last_incoming, stash = lax.fori_loop(0, steps_total, forward_step, (zero_act, stash_init))
    normed_init = stash["normed"]
    grad_init = jnp.zeros((num_batches, tokens, width), jnp.bfloat16)

    def backward_step(step, carry):
        incoming, normed_buf, grad_buf = carry
        batch = step - (num_sections - 1 - section_pos)
        valid = jnp.logical_and(batch >= 0, batch < num_batches)
        slot = jnp.clip(batch, 0, num_batches - 1)

        def backward_compute(buffers):
            normed_now, grad_now = buffers
            state = pick(stash["states"], slot)
            normed = pick(normed_now, slot)
            preact = pick(stash["preact"], slot)
            result = state + activate(preact)
            upstream = jnp.where(is_last, result * loss_scale, incoming.astype(jnp.float32))
            grad_pre = jax.vjp(activate, preact)[1](upstream)[0].astype(jnp.bfloat16)
            grad_normed = lax.dot_general(
                grad_pre, layer_weight, (((1,), (1,)), ((), ())), preferred_element_type=jnp.float32
            )
            norm_map = partial(normalize, norm_gain=layer_gain)
            grad_state = upstream + jax.vjp(norm_map, state)[1](grad_normed)[0]
            sent = grad_state.astype(jnp.bfloat16)
            return (sent, (place(normed_now, normed, slot), place(grad_now, grad_pre, slot)))

        def backward_skip(buffers):
            return (zero_act, buffers)

        sent, buffers = lax.cond(valid, backward_compute, backward_skip, (normed_buf, grad_buf))
        outgoing = from_behind(sent, "section", -1)
        return (outgoing, buffers[0], buffers[1])

    unused_grad, normed_buf, grad_buf = lax.fori_loop(
        0, steps_total, backward_step, (zero_act, normed_init, grad_init)
    )
    normed_rows = normed_buf.reshape(rows_total, width)
    grad_rows = grad_buf.reshape(rows_total, width)
    summed = lax.psum_scatter(
        lax.dot_general(
            normed_rows, grad_rows, (((0,), (0,)), ((), ())), preferred_element_type=jnp.float32
        ).astype(jnp.bfloat16),
        "dp",
        scatter_dimension=0,
        tiled=True,
    )
    return (stash["results"][None], summed[None])


def solution(mesh):
    return jax.shard_map(
        per_device,
        mesh=mesh,
        in_specs=(
            P("dp", None, None),
            P("dp", None),
            P("section", None, "dp", None, None),
            P("section", None, None),
            P("section", None),
        ),
        out_specs=(P("section", "dp", None, None), P("section", "dp", None)),
        check_vma=False,
    )
```

profile of v0, /device:TPU:8, one launch (start us, length us, event | category | flops | bytes accessed | tf_op | source)
XLA Modules:
  0.0 950.9 jit_solution(9967154390848724778)
XLA Ops:
  7.2 3.8 slice_bitcast_fusion
  17.1 301.6 %while.40 = (s32[]{:T(128)}, bf16[128,3072]{1,0:T(8,128)(2,1)}, bf16[2,128,3072]{2,1,0:T(8,128)(2,1)}, f32[2,128,3072]{2,1,0:T(8,128)}, bf16[2,128,3072]{2,1,0:T...) while((s32[]{:T(128)}, bf16[128,3072]{1,0:T(8,128)(2,1)}, ...), condition=%wide.region_5.6_spmd, body=%wide.region_0.5_spmd.sunk | while | flops 2450129152 | bytes 82606184 | solution.py:97
  18.0 3.3 collective-permute-start
  21.3 37.9 %collective-permute-done = bf16[128,3072]{1,0:T(8,128)(2,1)} collective-permute-done((bf16[128,3072]{1,0:T(8,128)(2,1)}, bf16[128,3072]{1,0:T(8,128)(2,1)}, u32[]{:S(2)}, u32[]{:S(2)}) %collective-permute-start) | collective-permute-done | bytes 786464 | tf_op jit(solution)/shard_map/while/body/eval_jaxpr/ppermute | solution.py:16
  59.2 23.4 %conditional.4 = (bf16[128,3072]{1,0:T(8,128)(2,1)}, bf16[2,128,3072]{2,1,0:T(8,128)(2,1)}, f32[2,128,3072]{2,1,0:T(8,128)}, bf16[2,128,3072]{2,1,0:T(8,128)(2,1)}, f32[2,128,3072]{2,1,0:T(8,128)S(1)}) conditional(s32[]{:T(128)} %convert_element_type.91, (bf16[2,128,3072]{2,1,0:T(8,128)(2,1)}, f32[2,128,3072]{2,1,0:T(8,128)}, ...), branch_computations={%region_1.1_spmd, %region_2.4_spmd} | conditional | flops 2450129152 | bytes 79460088 | solution.py:93
  61.8 3.2 bitcast_dynamic-update-slice_fusion
  68.4 11.0 %bitcast_dynamic-update-slice_fusion.2 = (bf16[2,128,3072]{2,1,0:T(8,128)(2,1)}, f32[128,3072]{1,0:T(8,128)S(1)}, bf16[2,128,3072]{2,1,0:T(8,128)(2,1)}, f32[128,3072]{1,0:T(8,128)S(1)}) fusion(bf16[2,128,3072]{2,1,0:T(8,128)(2,1)} %get-tuple-element.559, s32[]{:T(128)S(6)} %min.23, f32[128,3072]{1,0:T(8,128)S(1)} %copy-done, ...), kind=kOutput, calls=%fused_computation.28 | convolution fusion | flops 2445017088 | bytes 26765316 | tf_op jit(solution)/shard_map/while/body/eval_jaxpr/cond/branch_1_fun/dot_general | solution.py:32
  84.6 18.3 %collective-permute-done = bf16[128,3072]{1,0:T(8,128)(2,1)} collective-permute-done((bf16[128,3072]{1,0:T(8,128)(2,1)}, bf16[128,3072]{1,0:T(8,128)(2,1)}, u32[]{:S(2)}, u32[]{:S(2)}) %collective-permute-start) | collective-permute-done | bytes 786464 | tf_op jit(solution)/shard_map/while/body/eval_jaxpr/ppermute | solution.py:16
  102.9 23.4 %conditional.4 = (bf16[128,3072]{1,0:T(8,128)(2,1)}, bf16[2,128,3072]{2,1,0:T(8,128)(2,1)}, f32[2,128,3072]{2,1,0:T(8,128)}, bf16[2,128,3072]{2,1,0:T(8,128)(2,1)}, f32[2,128,3072]{2,1,0:T(8,128)S(1)}) conditional(s32[]{:T(128)} %convert_element_type.91, (bf16[2,128,3072]{2,1,0:T(8,128)(2,1)}, f32[2,128,3072]{2,1,0:T(8,128)}, ...), branch_computations={%region_1.1_spmd, %region_2.4_spmd} | conditional | flops 2450129152 | bytes 79460088 | solution.py:93
  105.4 3.2 bitcast_dynamic-update-slice_fusion
  112.0 11.0 %bitcast_dynamic-update-slice_fusion.2 = (bf16[2,128,3072]{2,1,0:T(8,128)(2,1)}, f32[128,3072]{1,0:T(8,128)S(1)}, bf16[2,128,3072]{2,1,0:T(8,128)(2,1)}, f32[128,3072]{1,0:T(8,128)S(1)}) fusion(bf16[2,128,3072]{2,1,0:T(8,128)(2,1)} %get-tuple-element.559, s32[]{:T(128)S(6)} %min.23, f32[128,3072]{1,0:T(8,128)S(1)} %copy-done, ...), kind=kOutput, calls=%fused_computation.28 | convolution fusion | flops 2445017088 | bytes 26765316 | tf_op jit(solution)/shard_map/while/body/eval_jaxpr/cond/branch_1_fun/dot_general | solution.py:32
  126.2 3.1 collective-permute-start
  129.4 16.2 %collective-permute-done = bf16[128,3072]{1,0:T(8,128)(2,1)} collective-permute-done((bf16[128,3072]{1,0:T(8,128)(2,1)}, bf16[128,3072]{1,0:T(8,128)(2,1)}, u32[]{:S(2)}, u32[]{:S(2)}) %collective-permute-start) | collective-permute-done | bytes 786464 | tf_op jit(solution)/shard_map/while/body/eval_jaxpr/ppermute | solution.py:16
  146.5 26.7 %collective-permute-start = (bf16[128,3072]{1,0:T(8,128)(2,1)}, bf16[128,3072]{1,0:T(8,128)(2,1)}, u32[]{:S(2)}, u32[]{:S(2)}) collective-permute-start(bf16[128,3072]{1,0:T(8,128)(2,1)} %get-tuple-element.830), channel_id=1, source_target_pairs={{0,16},{16,32},{32,48},{48,64},{64,80},{80,96},{96,112},{1,17},{17... | collective-permute-start | bytes 2359304 | tf_op jit(solution)/shard_map/while/body/eval_jaxpr/ppermute | solution.py:16
  173.3 14.4 %collective-permute-done = bf16[128,3072]{1,0:T(8,128)(2,1)} collective-permute-done((bf16[128,3072]{1,0:T(8,128)(2,1)}, bf16[128,3072]{1,0:T(8,128)(2,1)}, u32[]{:S(2)}, u32[]{:S(2)}) %collective-permute-start) | collective-permute-done | bytes 786464 | tf_op jit(solution)/shard_map/while/body/eval_jaxpr/ppermute | solution.py:16
  188.6 5.3 collective-permute-start
  193.9 13.5 %collective-permute-done = bf16[128,3072]{1,0:T(8,128)(2,1)} collective-permute-done((bf16[128,3072]{1,0:T(8,128)(2,1)}, bf16[128,3072]{1,0:T(8,128)(2,1)}, u32[]{:S(2)}, u32[]{:S(2)}) %collective-permute-start) | collective-permute-done | bytes 786464 | tf_op jit(solution)/shard_map/while/body/eval_jaxpr/ppermute | solution.py:16
  208.3 24.0 %collective-permute-start = (bf16[128,3072]{1,0:T(8,128)(2,1)}, bf16[128,3072]{1,0:T(8,128)(2,1)}, u32[]{:S(2)}, u32[]{:S(2)}) collective-permute-start(bf16[128,3072]{1,0:T(8,128)(2,1)} %get-tuple-element.830), channel_id=1, source_target_pairs={{0,16},{16,32},{32,48},{48,64},{64,80},{80,96},{96,112},{1,17},{17... | collective-permute-start | bytes 2359304 | tf_op jit(solution)/shard_map/while/body/eval_jaxpr/ppermute | solution.py:16
  232.4 12.9 %collective-permute-done = bf16[128,3072]{1,0:T(8,128)(2,1)} collective-permute-done((bf16[128,3072]{1,0:T(8,128)(2,1)}, bf16[128,3072]{1,0:T(8,128)(2,1)}, u32[]{:S(2)}, u32[]{:S(2)}) %collective-permute-start) | collective-permute-done | bytes 786464 | tf_op jit(solution)/shard_map/while/body/eval_jaxpr/ppermute | solution.py:16
  246.2 5.3 collective-permute-start
  251.5 12.1 %collective-permute-done = bf16[128,3072]{1,0:T(8,128)(2,1)} collective-permute-done((bf16[128,3072]{1,0:T(8,128)(2,1)}, bf16[128,3072]{1,0:T(8,128)(2,1)}, u32[]{:S(2)}, u32[]{:S(2)}) %collective-permute-start) | collective-permute-done | bytes 786464 | tf_op jit(solution)/shard_map/while/body/eval_jaxpr/ppermute | solution.py:16
  264.6 25.7 %collective-permute-start = (bf16[128,3072]{1,0:T(8,128)(2,1)}, bf16[128,3072]{1,0:T(8,128)(2,1)}, u32[]{:S(2)}, u32[]{:S(2)}) collective-permute-start(bf16[128,3072]{1,0:T(8,128)(2,1)} %get-tuple-element.830), channel_id=1, source_target_pairs={{0,16},{16,32},{32,48},{48,64},{64,80},{80,96},{96,112},{1,17},{17... | collective-permute-start | bytes 2359304 | tf_op jit(solution)/shard_map/while/body/eval_jaxpr/ppermute | solution.py:16
  290.3 11.5 %collective-permute-done = bf16[128,3072]{1,0:T(8,128)(2,1)} collective-permute-done((bf16[128,3072]{1,0:T(8,128)(2,1)}, bf16[128,3072]{1,0:T(8,128)(2,1)}, u32[]{:S(2)}, u32[]{:S(2)}) %collective-permute-start) | collective-permute-done | bytes 786464 | tf_op jit(solution)/shard_map/while/body/eval_jaxpr/ppermute | solution.py:16
  302.8 5.3 collective-permute-start
  308.1 10.6 %collective-permute-done = bf16[128,3072]{1,0:T(8,128)(2,1)} collective-permute-done((bf16[128,3072]{1,0:T(8,128)(2,1)}, bf16[128,3072]{1,0:T(8,128)(2,1)}, u32[]{:S(2)}, u32[]{:S(2)}) %collective-permute-start) | collective-permute-done | bytes 786464 | tf_op jit(solution)/shard_map/while/body/eval_jaxpr/ppermute | solution.py:16
  321.0 445.8 %while.41 = (s32[]{:T(128)}, bf16[128,3072]{1,0:T(8,128)(2,1)}, bf16[2,128,3072]{2,1,0:T(8,128)(2,1)}, bf16[2,128,3072]{2,1,0:T(8,128)(2,1)}, s32[]{:T(128)}, /*...) while((s32[]{:T(128)}, bf16[128,3072]{1,0:T(8,128)(2,1)}, ...), condition=%wide.region_13.14_spmd, body=%wide.region_6.13_spmd.sunk | while | flops 2454848256 | bytes 80238032 | solution.py:130
  323.9 33.8 %collective-permute-done.1 = bf16[128,3072]{1,0:T(8,128)(2,1)} collective-permute-done((bf16[128,3072]{1,0:T(8,128)(2,1)}, bf16[128,3072]{1,0:T(8,128)(2,1)}, u32[]{:S(2)}, u32[]{:S(2)}) %collective-permute-start.1) | collective-permute-done | bytes 786464 | tf_op jit(solution)/shard_map/while/body/eval_jaxpr/ppermute | solution.py:16
  360.6 13.6 %collective-permute-done.1 = bf16[128,3072]{1,0:T(8,128)(2,1)} collective-permute-done((bf16[128,3072]{1,0:T(8,128)(2,1)}, bf16[128,3072]{1,0:T(8,128)(2,1)}, u32[]{:S(2)}, u32[]{:S(2)}) %collective-permute-start.1) | collective-permute-done | bytes 786464 | tf_op jit(solution)/shard_map/while/body/eval_jaxpr/ppermute | solution.py:16
  377.1 35.6 %collective-permute-done.1 = bf16[128,3072]{1,0:T(8,128)(2,1)} collective-permute-done((bf16[128,3072]{1,0:T(8,128)(2,1)}, bf16[128,3072]{1,0:T(8,128)(2,1)}, u32[]{:S(2)}, u32[]{:S(2)}) %collective-permute-start.1) | collective-permute-done | bytes 786464 | tf_op jit(solution)/shard_map/while/body/eval_jaxpr/ppermute | solution.py:16
  415.5 13.2 %collective-permute-done.1 = bf16[128,3072]{1,0:T(8,128)(2,1)} collective-permute-done((bf16[128,3072]{1,0:T(8,128)(2,1)}, bf16[128,3072]{1,0:T(8,128)(2,1)}, u32[]{:S(2)}, u32[]{:S(2)}) %collective-permute-start.1) | collective-permute-done | bytes 786464 | tf_op jit(solution)/shard_map/while/body/eval_jaxpr/ppermute | solution.py:16
  429.7 2.7 collective-permute-start.1
  432.4 31.3 %collective-permute-done.1 = bf16[128,3072]{1,0:T(8,128)(2,1)} collective-permute-done((bf16[128,3072]{1,0:T(8,128)(2,1)}, bf16[128,3072]{1,0:T(8,128)(2,1)}, u32[]{:S(2)}, u32[]{:S(2)}) %collective-permute-start.1) | collective-permute-done | bytes 786464 | tf_op jit(solution)/shard_map/while/body/eval_jaxpr/ppermute | solution.py:16
  466.5 174.9 %collective-permute-done.1 = bf16[128,3072]{1,0:T(8,128)(2,1)} collective-permute-done((bf16[128,3072]{1,0:T(8,128)(2,1)}, bf16[128,3072]{1,0:T(8,128)(2,1)}, u32[]{:S(2)}, u32[]{:S(2)}) %collective-permute-start.1) | collective-permute-done | bytes 786464 | tf_op jit(solution)/shard_map/while/body/eval_jaxpr/ppermute | solution.py:16
  641.5 28.1 %conditional.5 = (bf16[128,3072]{1,0:T(8,128)(2,1)}, bf16[2,128,3072]{2,1,0:T(8,128)(2,1)}, bf16[2,128,3072]{2,1,0:T(8,128)(2,1)}) conditional(s32[]{:T(128)} %convert_element_type.92, (bf16[2,128,3072]{2,1,0:T(8,128)(2,1)}, bf16[2,128,3072]{2,1,0:T(8,128)(2,1)}) %tuple.97, (pred[]{:T(512)}, s32[]{:T(128)}, f32[2,128,3072]{2,1,0:T(8,128)S(1)}, ...), branch_computations={%region_7.7_spmd, %region_8.12_spmd} | conditional | flops 2454848256 | bytes 77092016 | solution.py:126
  641.5 6.9 bitcast_dynamic-update-slice_fusion.4
  648.5 14.1 %multiply_reduce_fusion.2 = (f32[128]{0:T(128)S(1)}, f32[128]{0:T(128)S(1)}, f32[128,3072]{1,0:T(8,128)}) fusion(f32[2,128,3072]{2,1,0:T(8,128)S(1)} %get-tuple-element.584, s32[]{:T(128)S(6)} %min.26, f32[128]{0:T(128)S(1)} %broadcast_multiply_fusion.1, f32[3072]{0:T(1024)S(1)} %bitcast.140, bf16[128,3072]{1,0:T(8,128)(2,1)} %get-tuple-element.675, ...), kind=kOutput, calls=%fused_computation.56 | convolution fusion | flops 2418278400 | bytes 22820356 | tf_op jit(solution)/shard_map/while/body/eval_jaxpr/cond/branch_1_fun/dot_general | solution.py:115
  662.7 2.0 fusion.42
  665.5 2.8 add_convert_fusion
  671.5 13.2 %collective-permute-done.1 = bf16[128,3072]{1,0:T(8,128)(2,1)} collective-permute-done((bf16[128,3072]{1,0:T(8,128)(2,1)}, bf16[128,3072]{1,0:T(8,128)(2,1)}, u32[]{:S(2)}, u32[]{:S(2)}) %collective-permute-start.1) | collective-permute-done | bytes 786464 | tf_op jit(solution)/shard_map/while/body/eval_jaxpr/ppermute | solution.py:16
  684.7 28.1 %conditional.5 = (bf16[128,3072]{1,0:T(8,128)(2,1)}, bf16[2,128,3072]{2,1,0:T(8,128)(2,1)}, bf16[2,128,3072]{2,1,0:T(8,128)(2,1)}) conditional(s32[]{:T(128)} %convert_element_type.92, (bf16[2,128,3072]{2,1,0:T(8,128)(2,1)}, bf16[2,128,3072]{2,1,0:T(8,128)(2,1)}) %tuple.97, (pred[]{:T(512)}, s32[]{:T(128)}, f32[2,128,3072]{2,1,0:T(8,128)S(1)}, ...), branch_computations={%region_7.7_spmd, %region_8.12_spmd} | conditional | flops 2454848256 | bytes 77092016 | solution.py:126
  684.7 6.9 bitcast_dynamic-update-slice_fusion.4
  691.7 14.1 %multiply_reduce_fusion.2 = (f32[128]{0:T(128)S(1)}, f32[128]{0:T(128)S(1)}, f32[128,3072]{1,0:T(8,128)}) fusion(f32[2,128,3072]{2,1,0:T(8,128)S(1)} %get-tuple-element.584, s32[]{:T(128)S(6)} %min.26, f32[128]{0:T(128)S(1)} %broadcast_multiply_fusion.1, f32[3072]{0:T(1024)S(1)} %bitcast.140, bf16[128,3072]{1,0:T(8,128)(2,1)} %get-tuple-element.675, ...), kind=kOutput, calls=%fused_computation.56 | convolution fusion | flops 2418278400 | bytes 22820356 | tf_op jit(solution)/shard_map/while/body/eval_jaxpr/cond/branch_1_fun/dot_general | solution.py:115
  708.6 2.8 add_convert_fusion
  714.7 20.1 %collective-permute-done.1 = bf16[128,3072]{1,0:T(8,128)(2,1)} collective-permute-done((bf16[128,3072]{1,0:T(8,128)(2,1)}, bf16[128,3072]{1,0:T(8,128)(2,1)}, u32[]{:S(2)}, u32[]{:S(2)}) %collective-permute-start.1) | collective-permute-done | bytes 786464 | tf_op jit(solution)/shard_map/while/body/eval_jaxpr/ppermute | solution.py:16
  735.7 21.2 %collective-permute-start.1 = (bf16[128,3072]{1,0:T(8,128)(2,1)}, bf16[128,3072]{1,0:T(8,128)(2,1)}, u32[]{:S(2)}, u32[]{:S(2)}) collective-permute-start(bf16[128,3072]{1,0:T(8,128)(2,1)} %get-tuple-element.845), channel_id=1, source_target_pairs={{16,0},{32,16},{48,32},{64,48},{80,64},{96,80},{112,96},{17,1},{33... | collective-permute-start | bytes 2359304 | tf_op jit(solution)/shard_map/while/body/eval_jaxpr/ppermute | solution.py:16
  756.9 9.8 %collective-permute-done.1 = bf16[128,3072]{1,0:T(8,128)(2,1)} collective-permute-done((bf16[128,3072]{1,0:T(8,128)(2,1)}, bf16[128,3072]{1,0:T(8,128)(2,1)}, u32[]{:S(2)}, u32[]{:S(2)}) %collective-permute-start.1) | collective-permute-done | bytes 786464 | tf_op jit(solution)/shard_map/while/body/eval_jaxpr/ppermute | solution.py:16
  766.7 11.0 %bitcast_convert_fusion = bf16[3072,3072]{1,0:T(8,128)(2,1)} fusion(bf16[2,128,3072]{2,1,0:T(8,128)(2,1)} %get-tuple-element.618, bf16[2,128,3072]{2,1,0:T(8,128)(2,1)} %get-tuple-element.619), kind=kOutput, calls=%fused_computation.78 | convolution fusion | flops 4841275392 | bytes 22020096 | tf_op jit(solution)/shard_map/dot_general | solution.py:136
  777.8 166.2 %reduce-scatter.2.cloned.1.call-done = bf16[192,3072]{1,0:T(8,128)(2,1)} async-done(((bf16[3072,3072]{1,0:T(8,128)(2,1)}), bf16[192,3072]{1,0:T(8,128)(2,1)}) %reduce-scatter.2.cloned.1.call-update) | async-done | bytes 1179664 | tf_op jit(solution)/shard_map/reduce_scatter | solution.py:135
  (106 shorter events, 71.5 us)
Async XLA Ops:
  7.2 936.8 %reduce-scatter.2.cloned.1.call-start = ((), (), s32[]{:S(2)}) async-start(), calls=%async_computation.1 | async-start | bytes 20054016 | tf_op jit(solution)/shard_map/reduce_scatter | solution.py:135
  14.7 2.4 copy-start.8
  14.7 2.4 copy-start.9
  18.0 41.2 %collective-permute-start = (bf16[128,3072]{1,0:T(8,128)(2,1)}, bf16[128,3072]{1,0:T(8,128)(2,1)}, u32[]{:S(2)}, u32[]{:S(2)}) collective-permute-start(bf16[128,3072]{1,0:T(8,128)(2,1)} %get-tuple-element.830), channel_id=1, source_target_pairs={{0,16},{16,32},{32,48},{48,64},{64,80},{80,96},{96,112},{1,17},{17... | collective-permute-start | bytes 2359304 | tf_op jit(solution)/shard_map/while/body/eval_jaxpr/ppermute | solution.py:16
  66.5 1.9 copy-start
  68.4 11.0 %copy-start.2 = (f32[2,128,3072]{2,1,0:T(8,128)S(1)}, f32[2,128,3072]{2,1,0:T(8,128)}, u32[]{:S(2)}) copy-start(f32[2,128,3072]{2,1,0:T(8,128)} %get-tuple-element.558) | copy-start | bytes 9437188 | tf_op jit(solution)/shard_map/while/body/eval_jaxpr/cond
  79.4 2.1 copy-start.7
  79.6 3.1 copy-start.3
  82.7 20.2 %collective-permute-start = (bf16[128,3072]{1,0:T(8,128)(2,1)}, bf16[128,3072]{1,0:T(8,128)(2,1)}, u32[]{:S(2)}, u32[]{:S(2)}) collective-permute-start(bf16[128,3072]{1,0:T(8,128)(2,1)} %get-tuple-element.830), channel_id=1, source_target_pairs={{0,16},{16,32},{32,48},{48,64},{64,80},{80,96},{96,112},{1,17},{17... | collective-permute-start | bytes 2359304 | tf_op jit(solution)/shard_map/while/body/eval_jaxpr/ppermute | solution.py:16
  110.1 1.9 copy-start
  112.0 11.0 %copy-start.2 = (f32[2,128,3072]{2,1,0:T(8,128)S(1)}, f32[2,128,3072]{2,1,0:T(8,128)}, u32[]{:S(2)}) copy-start(f32[2,128,3072]{2,1,0:T(8,128)} %get-tuple-element.558) | copy-start | bytes 9437188 | tf_op jit(solution)/shard_map/while/body/eval_jaxpr/cond
  123.0 2.1 copy-start.7
  123.2 3.1 copy-start.3
  126.2 19.3 %collective-permute-start = (bf16[128,3072]{1,0:T(8,128)(2,1)}, bf16[128,3072]{1,0:T(8,128)(2,1)}, u32[]{:S(2)}, u32[]{:S(2)}) collective-permute-start(bf16[128,3072]{1,0:T(8,128)(2,1)} %get-tuple-element.830), channel_id=1, source_target_pairs={{0,16},{16,32},{32,48},{48,64},{64,80},{80,96},{96,112},{1,17},{17... | collective-permute-start | bytes 2359304 | tf_op jit(solution)/shard_map/while/body/eval_jaxpr/ppermute | solution.py:16
  146.5 41.1 %collective-permute-start = (bf16[128,3072]{1,0:T(8,128)(2,1)}, bf16[128,3072]{1,0:T(8,128)(2,1)}, u32[]{:S(2)}, u32[]{:S(2)}) collective-permute-start(bf16[128,3072]{1,0:T(8,128)(2,1)} %get-tuple-element.830), channel_id=1, source_target_pairs={{0,16},{16,32},{32,48},{48,64},{64,80},{80,96},{96,112},{1,17},{17... | collective-permute-start | bytes 2359304 | tf_op jit(solution)/shard_map/while/body/eval_jaxpr/ppermute | solution.py:16
  188.6 18.8 %collective-permute-start = (bf16[128,3072]{1,0:T(8,128)(2,1)}, bf16[128,3072]{1,0:T(8,128)(2,1)}, u32[]{:S(2)}, u32[]{:S(2)}) collective-permute-start(bf16[128,3072]{1,0:T(8,128)(2,1)} %get-tuple-element.830), channel_id=1, source_target_pairs={{0,16},{16,32},{32,48},{48,64},{64,80},{80,96},{96,112},{1,17},{17... | collective-permute-start | bytes 2359304 | tf_op jit(solution)/shard_map/while/body/eval_jaxpr/ppermute | solution.py:16
  208.3 36.9 %collective-permute-start = (bf16[128,3072]{1,0:T(8,128)(2,1)}, bf16[128,3072]{1,0:T(8,128)(2,1)}, u32[]{:S(2)}, u32[]{:S(2)}) collective-permute-start(bf16[128,3072]{1,0:T(8,128)(2,1)} %get-tuple-element.830), channel_id=1, source_target_pairs={{0,16},{16,32},{32,48},{48,64},{64,80},{80,96},{96,112},{1,17},{17... | collective-permute-start | bytes 2359304 | tf_op jit(solution)/shard_map/while/body/eval_jaxpr/ppermute | solution.py:16
  246.2 17.4 %collective-permute-start = (bf16[128,3072]{1,0:T(8,128)(2,1)}, bf16[128,3072]{1,0:T(8,128)(2,1)}, u32[]{:S(2)}, u32[]{:S(2)}) collective-permute-start(bf16[128,3072]{1,0:T(8,128)(2,1)} %get-tuple-element.830), channel_id=1, source_target_pairs={{0,16},{16,32},{32,48},{48,64},{64,80},{80,96},{96,112},{1,17},{17... | collective-permute-start | bytes 2359304 | tf_op jit(solution)/shard_map/while/body/eval_jaxpr/ppermute | solution.py:16
  264.6 37.2 %collective-permute-start = (bf16[128,3072]{1,0:T(8,128)(2,1)}, bf16[128,3072]{1,0:T(8,128)(2,1)}, u32[]{:S(2)}, u32[]{:S(2)}) collective-permute-start(bf16[128,3072]{1,0:T(8,128)(2,1)} %get-tuple-element.830), channel_id=1, source_target_pairs={{0,16},{16,32},{32,48},{48,64},{64,80},{80,96},{96,112},{1,17},{17... | collective-permute-start | bytes 2359304 | tf_op jit(solution)/shard_map/while/body/eval_jaxpr/ppermute | solution.py:16
  302.8 15.9 %collective-permute-start = (bf16[128,3072]{1,0:T(8,128)(2,1)}, bf16[128,3072]{1,0:T(8,128)(2,1)}, u32[]{:S(2)}, u32[]{:S(2)}) collective-permute-start(bf16[128,3072]{1,0:T(8,128)(2,1)} %get-tuple-element.830), channel_id=1, source_target_pairs={{0,16},{16,32},{32,48},{48,64},{64,80},{80,96},{96,112},{1,17},{17... | collective-permute-start | bytes 2359304 | tf_op jit(solution)/shard_map/while/body/eval_jaxpr/ppermute | solution.py:16
  322.0 35.7 %collective-permute-start.1 = (bf16[128,3072]{1,0:T(8,128)(2,1)}, bf16[128,3072]{1,0:T(8,128)(2,1)}, u32[]{:S(2)}, u32[]{:S(2)}) collective-permute-start(bf16[128,3072]{1,0:T(8,128)(2,1)} %get-tuple-element.845), channel_id=1, source_target_pairs={{16,0},{32,16},{48,32},{64,48},{80,64},{96,80},{112,96},{17,1},{33... | collective-permute-start | bytes 2359304 | tf_op jit(solution)/shard_map/while/body/eval_jaxpr/ppermute | solution.py:16
  358.7 15.5 %collective-permute-start.1 = (bf16[128,3072]{1,0:T(8,128)(2,1)}, bf16[128,3072]{1,0:T(8,128)(2,1)}, u32[]{:S(2)}, u32[]{:S(2)}) collective-permute-start(bf16[128,3072]{1,0:T(8,128)(2,1)} %get-tuple-element.845), channel_id=1, source_target_pairs={{16,0},{32,16},{48,32},{64,48},{80,64},{96,80},{112,96},{17,1},{33... | collective-permute-start | bytes 2359304 | tf_op jit(solution)/shard_map/while/body/eval_jaxpr/ppermute | solution.py:16
  375.1 37.5 %collective-permute-start.1 = (bf16[128,3072]{1,0:T(8,128)(2,1)}, bf16[128,3072]{1,0:T(8,128)(2,1)}, u32[]{:S(2)}, u32[]{:S(2)}) collective-permute-start(bf16[128,3072]{1,0:T(8,128)(2,1)} %get-tuple-element.845), channel_id=1, source_target_pairs={{16,0},{32,16},{48,32},{64,48},{80,64},{96,80},{112,96},{17,1},{33... | collective-permute-start | bytes 2359304 | tf_op jit(solution)/shard_map/while/body/eval_jaxpr/ppermute | solution.py:16
  413.6 15.1 %collective-permute-start.1 = (bf16[128,3072]{1,0:T(8,128)(2,1)}, bf16[128,3072]{1,0:T(8,128)(2,1)}, u32[]{:S(2)}, u32[]{:S(2)}) collective-permute-start(bf16[128,3072]{1,0:T(8,128)(2,1)} %get-tuple-element.845), channel_id=1, source_target_pairs={{16,0},{32,16},{48,32},{64,48},{80,64},{96,80},{112,96},{17,1},{33... | collective-permute-start | bytes 2359304 | tf_op jit(solution)/shard_map/while/body/eval_jaxpr/ppermute | solution.py:16
  429.7 34.0 %collective-permute-start.1 = (bf16[128,3072]{1,0:T(8,128)(2,1)}, bf16[128,3072]{1,0:T(8,128)(2,1)}, u32[]{:S(2)}, u32[]{:S(2)}) collective-permute-start(bf16[128,3072]{1,0:T(8,128)(2,1)} %get-tuple-element.845), channel_id=1, source_target_pairs={{16,0},{32,16},{48,32},{64,48},{80,64},{96,80},{112,96},{17,1},{33... | collective-permute-start | bytes 2359304 | tf_op jit(solution)/shard_map/while/body/eval_jaxpr/ppermute | solution.py:16
  464.6 176.9 %collective-permute-start.1 = (bf16[128,3072]{1,0:T(8,128)(2,1)}, bf16[128,3072]{1,0:T(8,128)(2,1)}, u32[]{:S(2)}, u32[]{:S(2)}) collective-permute-start(bf16[128,3072]{1,0:T(8,128)(2,1)} %get-tuple-element.845), channel_id=1, source_target_pairs={{16,0},{32,16},{48,32},{64,48},{80,64},{96,80},{112,96},{17,1},{33... | collective-permute-start | bytes 2359304 | tf_op jit(solution)/shard_map/while/body/eval_jaxpr/ppermute | solution.py:16
  662.6 2.0 copy-start.1
  662.6 2.8 copy-start.4
  665.5 2.8 copy-start.5
  668.4 1.2 copy-start.6
  669.6 15.1 %collective-permute-start.1 = (bf16[128,3072]{1,0:T(8,128)(2,1)}, bf16[128,3072]{1,0:T(8,128)(2,1)}, u32[]{:S(2)}, u32[]{:S(2)}) collective-permute-start(bf16[128,3072]{1,0:T(8,128)(2,1)} %get-tuple-element.845), channel_id=1, source_target_pairs={{16,0},{32,16},{48,32},{64,48},{80,64},{96,80},{112,96},{17,1},{33... | collective-permute-start | bytes 2359304 | tf_op jit(solution)/shard_map/while/body/eval_jaxpr/ppermute | solution.py:16
  705.8 2.0 copy-start.1
  705.8 2.8 copy-start.4
  708.6 2.8 copy-start.5
  711.6 1.2 copy-start.6
  712.8 22.0 %collective-permute-start.1 = (bf16[128,3072]{1,0:T(8,128)(2,1)}, bf16[128,3072]{1,0:T(8,128)(2,1)}, u32[]{:S(2)}, u32[]{:S(2)}) collective-permute-start(bf16[128,3072]{1,0:T(8,128)(2,1)} %get-tuple-element.845), channel_id=1, source_target_pairs={{16,0},{32,16},{48,32},{64,48},{80,64},{96,80},{112,96},{17,1},{33... | collective-permute-start | bytes 2359304 | tf_op jit(solution)/shard_map/while/body/eval_jaxpr/ppermute | solution.py:16
  735.7 31.0 %collective-permute-start.1 = (bf16[128,3072]{1,0:T(8,128)(2,1)}, bf16[128,3072]{1,0:T(8,128)(2,1)}, u32[]{:S(2)}, u32[]{:S(2)}) collective-permute-start(bf16[128,3072]{1,0:T(8,128)(2,1)} %get-tuple-element.845), channel_id=1, source_target_pairs={{16,0},{32,16},{48,32},{64,48},{80,64},{96,80},{112,96},{17,1},{33... | collective-permute-start | bytes 2359304 | tf_op jit(solution)/shard_map/while/body/eval_jaxpr/ppermute | solution.py:16
Sparse Core Ops, SparseCore 0:
  777.9 166.0 reduce-scatter.1
where the time goes:
time: 953 us; the launch traced here: 951 us
  waiting for transfers between devices  659 us (69%)
  starting transfers between devices  138 us (14%)
  matrix products  61.2 us (6%)
  other arithmetic  39.1 us (4%)
  local copies, waits for them, and re-layouts  35.1 us (4%)
  between operations  14.1 us (1%)
    ppermute x18, waiting for transfers between devices, from_behind(): return lax.ppermute(shard, axis, pairs)  493 us
    reduce_scatter x1, waiting for transfers between devices, per_device(): lax.psum_scatter(lax.dot_general(normed_rows, grad_rows, (((0,), (0,)), (...  166 us
    ppermute x18, starting transfers between devices, from_behind(): return lax.ppermute(shard, axis, pairs)  138 us
    dot_general x2, matrix products, backward_compute(): lax.dot_general(grad_pre, layer_weight, (((1,), (1,)), ((), ())), preferr...  28.2 us
    dot_general x2, matrix products, forward_layer(): preact = jnp.dot(normed, layer_weight, preferred_element_type=jnp.float32)  22 us
    dynamic_update_slice x4, other arithmetic, place(): return lax.dynamic_update_index_in_dim(table, value, index, 0)  20.1 us
  transfers between devices with their start and end apart: 19, of which 19 were waited for; matrix products, arithmetic and copies ran while one was open for 0% of the time, Pallas kernels for 0%

commit v1 on v0

v1 whole, which is shorter than its diff:
```python
import functools
import math

import jax
import jax.numpy as jnp
from jax import lax
from jax.experimental import pallas as pl
from jax.experimental.pallas import tpu as pltpu
from jax.sharding import PartitionSpec as P

epsilon = 1e-05
delta_bound = 2.0
CHUNK = 32
PIECES = 4
MESH = pl.DeviceIdType.MESH
f32 = jnp.float32
bf16 = jnp.bfloat16
rsqrt2 = 1.0 / math.sqrt(2.0)
rsqrt2pi = 1.0 / math.sqrt(2.0 * math.pi)


def relay_kernel(
    scale,
    ids_ref, inputs_hbm, stored_hbm, w_hbm, gain_ref,
    out_hbm, normed_hbm, grad_hbm,
    w_v, base_v, keep_v, fin_v, clip_v, normed_v, pre_v, out_v, bin_v, bout_v, gp_v,
    acc_v, up_v, mu_v, rs_v,
    sem_w, sem_base, sem_keep, fsend, frecv, bsend, brecv, sem_out, sem_nrm, sem_gp,
):
    s = lax.axis_index("section")
    sections = lax.axis_size("section")
    last = sections - 1
    chunks, rows, width = fin_v.shape
    tokens = base_v.shape[1]
    per_batch = tokens // rows
    block = width // PIECES
    has_next = s < last
    has_prev = s > 0
    nxt = {"section": jnp.minimum(s + 1, last)}
    prv = {"section": jnp.maximum(s - 1, 0)}

    pltpu.make_async_copy(w_hbm.at[0], w_v, sem_w).start()

    @pl.when(s == 0)
    def _():
        pltpu.make_async_copy(inputs_hbm, base_v, sem_base).start()

    @pl.when(has_prev)
    def _():
        pltpu.make_async_copy(stored_hbm.at[0, 0], base_v, sem_base).start()

    pltpu.make_async_copy(stored_hbm.at[0, 1], keep_v, sem_keep).start()

    barrier = pltpu.get_barrier_semaphore()

    @pl.when(has_next)
    def _():
        pl.semaphore_signal(barrier, inc=1, device_id=nxt, device_id_type=MESH)

    @pl.when(has_prev)
    def _():
        pl.semaphore_signal(barrier, inc=1, device_id=prv, device_id_type=MESH)

    pl.semaphore_wait(barrier, jnp.minimum(s, 1) + jnp.minimum(last - s, 1))

    @pl.when(s == 0)
    def _():
        fin_v[...] = jnp.zeros_like(fin_v)

    @pl.when(s == last)
    def _():
        bin_v[...] = jnp.zeros_like(bin_v)

    pltpu.make_async_copy(inputs_hbm, base_v, sem_base).wait()
    pltpu.make_async_copy(stored_hbm.at[0, 1], keep_v, sem_keep).wait()
    pltpu.make_async_copy(w_hbm.at[0], w_v, sem_w).wait()

    def cols_of(j):
        return pl.ds(pl.multiple_of(j * block, block), block)

    def fcopy(c, cols):
        return pltpu.make_async_remote_copy(
            src_ref=clip_v.at[c, :, cols], dst_ref=fin_v.at[c, :, cols],
            send_sem=fsend.at[c], recv_sem=frecv.at[c], device_id=nxt, device_id_type=MESH)

    def fwhole(c):
        return pltpu.make_async_remote_copy(
            src_ref=clip_v.at[c], dst_ref=fin_v.at[c],
            send_sem=fsend.at[c], recv_sem=frecv.at[c], device_id=nxt, device_id_type=MESH)

    def bcopy(c, j):
        cols = cols_of(j)
        return pltpu.make_async_remote_copy(
            src_ref=bout_v.at[c, :, cols], dst_ref=bin_v.at[c, :, cols],
            send_sem=bsend.at[c, j], recv_sem=brecv.at[c, j], device_id=prv, device_id_type=MESH)

    def place(c):
        batch = c // per_batch
        first = pl.multiple_of((c % per_batch) * rows, rows)
        sample = ids_ref[0, batch]
        index = jnp.where(s == 0, batch, sample)
        return batch, first, sample, index

    def forward(c, carry):
        batch, first, sample, index = place(c)

        @pl.when(has_prev)
        def _():
            fwhole(c).wait_recv()

        x = base_v[index, pl.ds(first, rows), :].astype(f32) + fin_v[c].astype(f32)
        mu = jnp.mean(x, axis=-1, keepdims=True)
        xc = x - mu
        var = jnp.mean(xc * xc, axis=-1, keepdims=True)
        rs = lax.rsqrt(var + epsilon)
        normed_v[c] = (xc * rs * gain_ref[...]).astype(bf16)
        mu_v[c] = jnp.broadcast_to(mu, (rows, 128))
        rs_v[c] = jnp.broadcast_to(rs, (rows, 128))

        def tile(j, carry2):
            cols = cols_of(j)
            v = jnp.dot(normed_v[c], w_v[:, cols], preferred_element_type=f32)
            pre_v[c, :, cols] = v
            state = base_v[index, pl.ds(first, rows), cols].astype(f32) + fin_v[c, :, cols].astype(f32)
            res = state + v * (0.5 + 0.5 * lax.erf(v * rsqrt2))
            out_v[c, :, cols] = res.astype(bf16)
            kept = keep_v[sample, pl.ds(first, rows), cols].astype(f32)
            clip_v[c, :, cols] = jnp.clip(res - kept, -delta_bound, delta_bound).astype(bf16)

            @pl.when(has_next)
            def _():
                fcopy(c, cols).start()

            return carry2

        lax.fori_loop(0, PIECES, tile, 0)
        pltpu.make_async_copy(out_v.at[c], out_hbm.at[batch, pl.ds(first, rows)], sem_out.at[c]).start()
        pltpu.make_async_copy(normed_v.at[c], normed_hbm.at[batch, pl.ds(first, rows)], sem_nrm.at[c]).start()
        return carry

    lax.fori_loop(0, chunks, forward, 0)

    def backward(c, carry):
        batch, first, sample, index = place(c)
        acc_v[...] = jnp.zeros_like(acc_v)

        def tile(j, carry2):
            cols = cols_of(j)

            @pl.when(has_next)
            def _():
                bcopy(c, j).wait_recv()

            v = pre_v[c, :, cols]
            cdf = 0.5 + 0.5 * lax.erf(v * rsqrt2)
            slope = cdf + v * (jnp.exp(-0.5 * v * v) * rsqrt2pi)
            state = base_v[index, pl.ds(first, rows), cols].astype(f32) + fin_v[c, :, cols].astype(f32)
            up = jnp.where(s == last, (state + v * cdf) * scale, bin_v[c, :, cols].astype(f32))
            up_v[:, cols] = up
            gp_v[c, :, cols] = (slope * up).astype(bf16)
            acc_v[...] += lax.dot_general(
                gp_v[c, :, cols], w_v[:, cols], (((1,), (1,)), ((), ())), preferred_element_type=f32)
            return carry2

        lax.fori_loop(0, PIECES, tile, 0)
        pltpu.make_async_copy(gp_v.at[c], grad_hbm.at[batch, pl.ds(first, rows)], sem_gp.at[c]).start()
        mu = mu_v[c][:, :1]
        rs = rs_v[c][:, :1]
        x = base_v[index, pl.ds(first, rows), :].astype(f32) + fin_v[c].astype(f32)
        xhat = (x - mu) * rs
        dx = acc_v[...] * gain_ref[...]
        m1 = jnp.mean(dx, axis=-1, keepdims=True)
        m2 = jnp.mean(dx * xhat, axis=-1, keepdims=True)
        bout_v[c] = (up_v[...] + rs * (dx - m1 - xhat * m2)).astype(bf16)

        @pl.when(has_prev)
        def _():
            for j in range(PIECES):
                bcopy(c, j).start()

        return carry

    lax.fori_loop(0, chunks, backward, 0)

    def finish(c, carry):
        batch, first, sample, index = place(c)
        pltpu.make_async_copy(out_v.at[c], out_hbm.at[batch, pl.ds(first, rows)], sem_out.at[c]).wait()
        pltpu.make_async_copy(normed_v.at[c], normed_hbm.at[batch, pl.ds(first, rows)], sem_nrm.at[c]).wait()
        pltpu.make_async_copy(gp_v.at[c], grad_hbm.at[batch, pl.ds(first, rows)], sem_gp.at[c]).wait()

        @pl.when(has_next)
        def _():
            fwhole(c).wait_send()

        @pl.when(has_prev)
        def _():
            for j in range(PIECES):
                bcopy(c, j).wait_send()

        return carry

    lax.fori_loop(0, chunks, finish, 0)


def relay(scale, inputs, sample_ids, stored, weight, norm_gain):
    batches, tokens, width = inputs.shape
    rows = min(CHUNK, tokens)
    chunks = batches * tokens // rows
    shape = jax.ShapeDtypeStruct(inputs.shape, bf16)
    any_spec = pl.BlockSpec(memory_space=pl.ANY)
    chunked = pltpu.VMEM((chunks, rows, width), bf16)
    dma = pltpu.SemaphoreType.DMA
    return pl.pallas_call(
        functools.partial(relay_kernel, scale),
        out_shape=(shape, shape, shape),
        in_specs=[
            pl.BlockSpec(memory_space=pltpu.SMEM), any_spec, any_spec, any_spec,
            pl.BlockSpec(memory_space=pltpu.VMEM),
        ],
        out_specs=(any_spec, any_spec, any_spec),
        scratch_shapes=[
            pltpu.VMEM((width, width), bf16),
            pltpu.VMEM(inputs.shape, bf16),
            pltpu.VMEM(inputs.shape, bf16),
            chunked, chunked, chunked,
            pltpu.VMEM((chunks, rows, width), f32),
            chunked, chunked, chunked, chunked,
            pltpu.VMEM((rows, width), f32),
            pltpu.VMEM((rows, width), f32),
            pltpu.VMEM((chunks, rows, 128), f32),
            pltpu.VMEM((chunks, rows, 128), f32),
            dma, dma, dma,
            dma((chunks,)), dma((chunks,)),
            dma((chunks, PIECES)), dma((chunks, PIECES)),
            dma((chunks,)), dma((chunks,)), dma((chunks,)),
        ],
        compiler_params=pltpu.CompilerParams(
            collective_id=0, has_side_effects=True, vmem_limit_bytes=60 * 1024 * 1024),
        cost_estimate=pl.CostEstimate(
            flops=4 * batches * tokens * width * width, bytes_accessed=2 * width * width, transcendentals=0),
        name="relay",
    )(sample_ids, inputs, stored, weight, norm_gain)


def per_device(inputs, sample_ids, stored, weight, norm_gain):
    batches, tokens, width = inputs.shape
    rows_total = batches * tokens
    scale = 1.0 / math.sqrt(lax.axis_size("dp") * rows_total)
    outs, normed, grads = relay(scale, inputs, sample_ids, stored, weight, norm_gain)
    summed = lax.psum_scatter(
        lax.dot_general(
            normed.reshape(rows_total, width), grads.reshape(rows_total, width),
            (((0,), (0,)), ((), ())), preferred_element_type=f32,
        ).astype(bf16),
        "dp", scatter_dimension=0, tiled=True,
    )
    return (outs[None], summed[None])


def solution(mesh):
    return jax.shard_map(
        per_device,
        mesh=mesh,
        in_specs=(
            P("dp", None, None),
            P("dp", None),
            P("section", None, "dp", None, None),
            P("section", None, None),
            P("section", None),
        ),
        out_specs=(P("section", "dp", None, None), P("section", "dp", None)),
        check_vma=False,
    )
```

time: 953 us -> 398 us (0.42)
  waiting for transfers between devices: 659 us -> 163 us
  Pallas kernels: 0 us -> 208 us
  starting transfers between devices: 138 us -> 0.04 us
  matrix products: 61.2 us -> 10.9 us
  other arithmetic: 39.1 us -> 0 us
  local copies, waits for them, and re-layouts: 35.1 us -> 1.15 us
    ppermute x18 -> x0, waiting for transfers between devices: 493 us -> none  [from_behind(): return lax.ppermute(shard, axis, pairs)]
    pallas_call x0 -> x1, Pallas kernels: none -> 208 us  [relay(): pl.pallas_call(functools.partial(relay_kernel, scale), out_shape=(shape,...]
    ppermute x18 -> x0, starting transfers between devices: 138 us -> none  [from_behind(): return lax.ppermute(shard, axis, pairs)]
    dot_general x5 -> x1, matrix products: 61.2 us -> 10.9 us  [per_device(): lax.dot_general(normed.reshape(rows_total, width), grads.reshape(rows_tot...]
    dynamic_update_slice x4 -> x0, other arithmetic: 20.1 us -> none  [place(): return lax.dynamic_update_index_in_dim(table, value, index, 0)]
    broadcast_in_dim x16 -> x0, local copies, waits for them, and re-layouts: 15.4 us -> none  [per_device(): zero_act = jnp.zeros((tokens, width), jnp.bfloat16)]
    reduce_sum x8 -> x0, other arithmetic: 11.2 us -> none  [the longest x2 4.04 us: normalize(): centred = state - average]
  transfers between devices with their start and end apart: 19 -> 1, of which waited for: 19 -> 1; matrix products, arithmetic and copies ran while one was open for 0% -> 0% of each run, Pallas kernels for 0% -> 0%
where the time goes in v1:
time: 398 us; the launch traced here: 397 us
  Pallas kernels  208 us (52%)
  waiting for transfers between devices  163 us (41%)
  between operations  14 us (4%)
  matrix products  10.9 us (3%)
    pallas_call x1, Pallas kernels, relay(): pl.pallas_call(functools.partial(relay_kernel, scale), out_shape=(shape,...  208 us
    reduce_scatter x1, waiting for transfers between devices, per_device(): lax.psum_scatter(lax.dot_general(normed.reshape(rows_total, width), grads...  163 us
    dot_general x1, matrix products, per_device(): lax.dot_general(normed.reshape(rows_total, width), grads.reshape(rows_tot...  10.9 us
  transfers between devices with their start and end apart: 1, of which 1 were waited for; matrix products, arithmetic and copies ran while one was open for 0% of the time, Pallas kernels for 0%

profile of v1, /device:TPU:8, one launch (start us, length us, event | category | flops | bytes accessed | tf_op | source)
XLA Modules:
  0.0 397.2 jit_solution(5611456956520314225)
XLA Ops:
  7.2 0.0 reduce-scatter.2.cloned.1.call-start
  7.2 208.4 %relay.1 = (bf16[2,128,3072]{2,1,0:T(8,128)(2,1)}, bf16[2,128,3072]{2,1,0:T(8,128)(2,1)}, bf16[2,128,3072]{2,1,0:T(8,128)(2,1)}) custom-call(s32[1,2]{1,0:T(1,128)} %ids_ref.1, bf16[2,128,3072]{2,1,0:T(8,128)(2,1)} %inputs_hbm.1, bf16[1,2,2,128,3072]{4,3,2,1,0:T(8,128)(2,1)} %stored_hbm.1, bf16[1,3072,3072]{2,1,0:T(8,128)(2,1)} %w_hbm.1, f32[1,3072]{1,0:T(1,128)} %gain_ref.1), custom_call_target="tpu_custom_call" | custom-call | flops 9663676416 | bytes 18874368 | tf_op jit(solution)/shard_map/relay/pallas_call | solution.py:213
  215.6 10.9 %bitcast_convert_fusion = bf16[3072,3072]{1,0:T(8,128)(2,1)} fusion(bf16[2,128,3072]{2,1,0:T(8,128)(2,1)} %get-tuple-element.6, bf16[2,128,3072]{2,1,0:T(8,128)(2,1)} %get-tuple-element.7), kind=kOutput, calls=%fused_computation | convolution fusion | flops 4841275392 | bytes 22020096 | tf_op jit(solution)/shard_map/dot_general | solution.py:251
  226.5 0.0 copy-start
  226.5 0.0 reduce-scatter.2.cloned.1.call-update
  226.5 162.7 %reduce-scatter.2.cloned.1.call-done = bf16[192,3072]{1,0:T(8,128)(2,1)} async-done(((bf16[3072,3072]{1,0:T(8,128)(2,1)}), bf16[192,3072]{1,0:T(8,128)(2,1)}) %reduce-scatter.2.cloned.1.call-update) | async-done | bytes 1179664 | tf_op jit(solution)/shard_map/reduce_scatter | solution.py:250
  389.2 0.0 copy-done
  389.2 1.1 copy.10
Async XLA Ops:
  7.2 382.1 %reduce-scatter.2.cloned.1.call-start = ((), (), s32[]{:S(2)}) async-start(), calls=%async_computation.1 | async-start | bytes 20054016 | tf_op jit(solution)/shard_map/reduce_scatter | solution.py:250
  226.5 162.7 %copy-start = (bf16[2,128,3072]{2,1,0:T(8,128)(2,1)S(1)}, bf16[2,128,3072]{2,1,0:T(8,128)(2,1)}, u32[]{:S(2)}) copy-start(bf16[2,128,3072]{2,1,0:T(8,128)(2,1)} %get-tuple-element.5) | copy-start | bytes 4718596
Sparse Core Ops, SparseCore 0:
  226.6 162.5 reduce-scatter.1

commit v2 on v1

v2 whole, which is shorter than its diff:
```python
import functools
import math

import jax
import jax.numpy as jnp
from jax import lax
from jax.experimental import pallas as pl
from jax.experimental.pallas import tpu as pltpu
from jax.sharding import PartitionSpec as P

epsilon = 1e-05
delta_bound = 2.0
CHUNK = 32
PIECES = 4
GRAD_PIECES = 6
MESH = pl.DeviceIdType.MESH
f32 = jnp.float32
bf16 = jnp.bfloat16
rsqrt2 = 1.0 / math.sqrt(2.0)
rsqrt2pi = 1.0 / math.sqrt(2.0 * math.pi)


def relay_kernel(
    scale,
    ids_ref, inputs_hbm, stored_hbm, w_hbm, gain_ref,
    out_hbm, wgrad_hbm,
    w_v, base_v, keep_v, fin_v, clip_v, normed_v, pre_v, out_v, bin_v, bout_v,
    acc_v, up_v, mu_v, rs_v,
    nt_v, ngat_v, ggat_v, tile_v, csend_v, crecv_v, own_v, ysend_v, yrecv_v, res_v,
    sem_w, sem_base, sem_keep, fsend, frecv, bsend, brecv, sem_out,
    nsend, nrecv, zsend, zrecv, csend, crecv, ysend, yrecv, sem_res,
):
    s = lax.axis_index("section")
    sections = lax.axis_size("section")
    d = lax.axis_index("dp")
    last = sections - 1
    chunks, rows, width = fin_v.shape
    tokens = base_v.shape[1]
    batches = base_v.shape[0]
    local = chunks * rows
    per_batch = tokens // rows
    block = width // PIECES
    has_next = s < last
    has_prev = s > 0
    nxt = {"section": jnp.minimum(s + 1, last)}
    prv = {"section": jnp.maximum(s - 1, 0)}
    z = d // 4
    rest = d % 4
    core = d % 2
    row = rest // 2
    z_up = (z + 1) % 4
    z_down = (z + 3) % 4
    z_far = (z + 2) % 4
    dev_up = {"dp": z_up * 4 + rest}
    dev_down = {"dp": z_down * 4 + rest}
    dev_far = {"dp": z_far * 4 + rest}
    dev_core = {"dp": d + 1 - 2 * core}
    dev_row = {"dp": z * 4 + (rest + 2) % 4}

    pltpu.make_async_copy(w_hbm.at[0], w_v, sem_w).start()

    @pl.when(s == 0)
    def _():
        pltpu.make_async_copy(inputs_hbm, base_v, sem_base).start()

    @pl.when(has_prev)
    def _():
        pltpu.make_async_copy(stored_hbm.at[0, 0], base_v, sem_base).start()

    pltpu.make_async_copy(stored_hbm.at[0, 1], keep_v, sem_keep).start()

    barrier = pltpu.get_barrier_semaphore()

    @pl.when(has_next)
    def _():
        pl.semaphore_signal(barrier, inc=1, device_id=nxt, device_id_type=MESH)

    @pl.when(has_prev)
    def _():
        pl.semaphore_signal(barrier, inc=1, device_id=prv, device_id_type=MESH)

    for peer in (dev_up, dev_down, dev_far, dev_core, dev_row):
        pl.semaphore_signal(barrier, inc=1, device_id=peer, device_id_type=MESH)
    pl.semaphore_wait(barrier, 5 + jnp.minimum(s, 1) + jnp.minimum(last - s, 1))

    @pl.when(s == 0)
    def _():
        fin_v[...] = jnp.zeros_like(fin_v)

    @pl.when(s == last)
    def _():
        bin_v[...] = jnp.zeros_like(bin_v)

    pltpu.make_async_copy(inputs_hbm, base_v, sem_base).wait()
    pltpu.make_async_copy(stored_hbm.at[0, 1], keep_v, sem_keep).wait()
    pltpu.make_async_copy(w_hbm.at[0], w_v, sem_w).wait()

    def remote(src, dst, send, recv, device):
        return pltpu.make_async_remote_copy(
            src_ref=src, dst_ref=dst, send_sem=send, recv_sem=recv, device_id=device, device_id_type=MESH)

    def cols_of(j):
        return pl.ds(pl.multiple_of(j * block, block), block)

    def fcopy(c, cols):
        return remote(clip_v.at[c, :, cols], fin_v.at[c, :, cols], fsend.at[c], frecv.at[c], nxt)

    def fwhole(c):
        return remote(clip_v.at[c], fin_v.at[c], fsend.at[c], frecv.at[c], nxt)

    def bcopy(c, j):
        cols = cols_of(j)
        return remote(bout_v.at[c, :, cols], bin_v.at[c, :, cols], bsend.at[c, j], brecv.at[c, j], prv)

    def place(c):
        batch = c // per_batch
        first = pl.multiple_of((c % per_batch) * rows, rows)
        sample = ids_ref[0, batch]
        index = jnp.where(s == 0, batch, sample)
        return batch, first, sample, index

    share = width // 4
    half = width // 2

    def slot_rows(slot, c):
        return pl.ds(pl.multiple_of(slot * local + c * rows, rows), rows)

    def to_up(c):
        return remote(ggat_v.at[slot_rows(0, c)], ggat_v.at[slot_rows(1, c)], zsend.at[0, c], zrecv.at[0, c], dev_up)

    def to_down(c):
        return remote(ggat_v.at[slot_rows(0, c)], ggat_v.at[slot_rows(2, c)], zsend.at[1, c], zrecv.at[1, c], dev_down)

    def pass_up(c):
        lanes = pl.ds(0, half)
        return remote(ggat_v.at[slot_rows(1, c), lanes], ggat_v.at[slot_rows(3, c), lanes],
                      zsend.at[2, c], zrecv.at[2, c], dev_up)

    def pass_down(c):
        lanes = pl.ds(half, half)
        return remote(ggat_v.at[slot_rows(2, c), lanes], ggat_v.at[slot_rows(3, c), lanes],
                      zsend.at[3, c], zrecv.at[3, c], dev_down)

    def pass_on(c):
        to_up(c).wait_recv()
        pass_up(c).start()
        to_down(c).wait_recv()
        pass_down(c).start()

    def ncopy(slot, z_to, device):
        return remote(nt_v.at[pl.ds(pl.multiple_of(z_to * share, share), share)],
                      ngat_v.at[:, pl.ds(slot * local, local)], nsend.at[slot - 1], nrecv.at[slot - 1], device)

    def share_normed():
        step = 256
        def turn(i, carry):
            cols = pl.ds(pl.multiple_of(i * step, step), step)
            for b in range(batches):
                values = normed_v[pl.ds(b * per_batch, per_batch), :, cols].reshape(tokens, step)
                nt_v[cols, pl.ds(b * tokens, tokens)] = values.T
            return carry
        lax.fori_loop(0, width // step, turn, 0)
        ncopy(1, z_up, dev_up).start()
        ncopy(2, z_down, dev_down).start()
        ncopy(3, z_far, dev_far).start()
        ngat_v[:, pl.ds(0, local)] = nt_v[pl.ds(pl.multiple_of(z * share, share), share)]

    def forward(c, carry):
        batch, first, sample, index = place(c)

        @pl.when(has_prev)
        def _():
            fwhole(c).wait_recv()

        x = base_v[index, pl.ds(first, rows), :].astype(f32) + fin_v[c].astype(f32)
        mu = jnp.mean(x, axis=-1, keepdims=True)
        xc = x - mu
        var = jnp.mean(xc * xc, axis=-1, keepdims=True)
        rs = lax.rsqrt(var + epsilon)
        normed_v[c] = (xc * rs * gain_ref[...]).astype(bf16)
        mu_v[c] = jnp.broadcast_to(mu, (rows, 128))
        rs_v[c] = jnp.broadcast_to(rs, (rows, 128))

        def tile(j, carry2):
            cols = cols_of(j)
            v = jnp.dot(normed_v[c], w_v[:, cols], preferred_element_type=f32)
            pre_v[c, :, cols] = v
            state = base_v[index, pl.ds(first, rows), cols].astype(f32) + fin_v[c, :, cols].astype(f32)
            res = state + v * (0.5 + 0.5 * lax.erf(v * rsqrt2))
            out_v[c, :, cols] = res.astype(bf16)
            kept = keep_v[sample, pl.ds(first, rows), cols].astype(f32)
            clip_v[c, :, cols] = jnp.clip(res - kept, -delta_bound, delta_bound).astype(bf16)

            @pl.when(has_next)
            def _():
                fcopy(c, cols).start()

            return carry2

        lax.fori_loop(0, PIECES, tile, 0)
        pltpu.make_async_copy(out_v.at[c], out_hbm.at[batch, pl.ds(first, rows)], sem_out.at[c]).start()
        return carry

    lax.fori_loop(0, chunks, forward, 0)

    @pl.when(has_next)
    def _():
        share_normed()

    def backward(c, carry):
        batch, first, sample, index = place(c)
        acc_v[...] = jnp.zeros_like(acc_v)

        def tile(j, carry2):
            cols = cols_of(j)

            @pl.when(has_next)
            def _():
                bcopy(c, j).wait_recv()

            v = pre_v[c, :, cols]
            cdf = 0.5 + 0.5 * lax.erf(v * rsqrt2)
            slope = cdf + v * (jnp.exp(-0.5 * v * v) * rsqrt2pi)
            state = base_v[index, pl.ds(first, rows), cols].astype(f32) + fin_v[c, :, cols].astype(f32)
            up = jnp.where(s == last, (state + v * cdf) * scale, bin_v[c, :, cols].astype(f32))
            up_v[:, cols] = up
            gp = (slope * up).astype(bf16)
            ggat_v[slot_rows(0, c), cols] = gp

            @pl.when(has_prev)
            def _():
                acc_v[...] += lax.dot_general(
                    gp, w_v[:, cols], (((1,), (1,)), ((), ())), preferred_element_type=f32)

            return carry2

        lax.fori_loop(0, PIECES, tile, 0)
        to_up(c).start()
        to_down(c).start()

        @pl.when(has_prev)
        def _():
            mu = mu_v[c][:, :1]
            rs = rs_v[c][:, :1]
            x = base_v[index, pl.ds(first, rows), :].astype(f32) + fin_v[c].astype(f32)
            xhat = (x - mu) * rs
            dx = acc_v[...] * gain_ref[...]
            m1 = jnp.mean(dx, axis=-1, keepdims=True)
            m2 = jnp.mean(dx * xhat, axis=-1, keepdims=True)
            bout_v[c] = (up_v[...] + rs * (dx - m1 - xhat * m2)).astype(bf16)
            for j in range(PIECES):
                bcopy(c, j).start()

        @pl.when(c >= 1)
        def _():
            pass_on(c - 1)

        return carry

    lax.fori_loop(0, chunks, backward, 0)
    pass_on(chunks - 1)

    @pl.when(s == last)
    def _():
        share_normed()

    def arrived(c, carry):
        pass_up(c).wait_recv()
        pass_down(c).wait_recv()
        return carry

    ncopy(1, z_up, dev_up).wait_recv()
    ncopy(2, z_down, dev_down).wait_recv()
    ncopy(3, z_far, dev_far).wait_recv()
    lax.fori_loop(0, chunks, arrived, 0)

    part = share // 4
    wide = width // GRAD_PIECES

    def lanes_of(q):
        return pl.ds(pl.multiple_of(q * wide, wide), wide)

    def core_copy(q):
        lanes = lanes_of(q)
        return remote(csend_v.at[:, :, lanes], crecv_v.at[:, :, lanes], csend.at[q], crecv.at[q], dev_core)

    def row_copy(q):
        lanes = lanes_of(q)
        return remote(ysend_v.at[:, lanes], yrecv_v.at[:, lanes], ysend.at[q], yrecv.at[q], dev_row)

    def res_copy(q):
        lanes = lanes_of(q)
        return pltpu.make_async_copy(res_v.at[:, lanes], wgrad_hbm.at[:, lanes], sem_res.at[q])

    def product(q, carry):
        @pl.when(q < GRAD_PIECES)
        def _():
            lanes = lanes_of(q)
            tile_v[...] = jnp.dot(ngat_v[...], ggat_v[:, lanes], preferred_element_type=f32)
            for y in range(2):
                mine = pl.ds(pl.multiple_of(y * 2 * part + core * part, part), part)
                other = pl.ds(pl.multiple_of(y * 2 * part + (1 - core) * part, part), part)
                csend_v[y, :, lanes] = tile_v[other, :].astype(bf16)
                own_v[y, :, lanes] = tile_v[mine, :]
            core_copy(q).start()

        @pl.when(q >= 1)
        def _():
            lanes = lanes_of(q - 1)
            core_copy(q - 1).wait_recv()
            ysend_v[:, lanes] = (own_v[1 - row, :, lanes] + crecv_v[1 - row, :, lanes].astype(f32)).astype(bf16)
            row_copy(q - 1).start()

        return carry

    lax.fori_loop(0, GRAD_PIECES + 1, product, 0)

    def total(q, carry):
        lanes = lanes_of(q)
        row_copy(q).wait_recv()
        res_v[:, lanes] = (
            own_v[row, :, lanes] + crecv_v[row, :, lanes].astype(f32) + yrecv_v[:, lanes].astype(f32)
        ).astype(bf16)
        res_copy(q).start()
        return carry

    lax.fori_loop(0, GRAD_PIECES, total, 0)

    def finish(c, carry):
        batch, first, sample, index = place(c)
        pltpu.make_async_copy(out_v.at[c], out_hbm.at[batch, pl.ds(first, rows)], sem_out.at[c]).wait()
        to_up(c).wait_send()
        to_down(c).wait_send()
        pass_up(c).wait_send()
        pass_down(c).wait_send()

        @pl.when(has_next)
        def _():
            fwhole(c).wait_send()

        @pl.when(has_prev)
        def _():
            for j in range(PIECES):
                bcopy(c, j).wait_send()

        return carry

    lax.fori_loop(0, chunks, finish, 0)

    def finish_grad(q, carry):
        core_copy(q).wait_send()
        row_copy(q).wait_send()
        res_copy(q).wait()
        return carry

    lax.fori_loop(0, GRAD_PIECES, finish_grad, 0)
    ncopy(1, z_up, dev_up).wait_send()
    ncopy(2, z_down, dev_down).wait_send()
    ncopy(3, z_far, dev_far).wait_send()


def relay(scale, inputs, sample_ids, stored, weight, norm_gain):
    batches, tokens, width = inputs.shape
    rows = min(CHUNK, tokens)
    local = batches * tokens
    chunks = local // rows
    share = width // 4
    part = share // 4
    any_spec = pl.BlockSpec(memory_space=pl.ANY)
    chunked = pltpu.VMEM((chunks, rows, width), bf16)
    dma = pltpu.SemaphoreType.DMA
    return pl.pallas_call(
        functools.partial(relay_kernel, scale),
        out_shape=(
            jax.ShapeDtypeStruct(inputs.shape, bf16),
            jax.ShapeDtypeStruct((part, width), bf16),
        ),
        in_specs=[
            pl.BlockSpec(memory_space=pltpu.SMEM), any_spec, any_spec, any_spec,
            pl.BlockSpec(memory_space=pltpu.VMEM),
        ],
        out_specs=(any_spec, any_spec),
        scratch_shapes=[
            pltpu.VMEM((width, width), bf16),
            pltpu.VMEM(inputs.shape, bf16),
            pltpu.VMEM(inputs.shape, bf16),
            chunked, chunked, chunked,
            pltpu.VMEM((chunks, rows, width), f32),
            chunked, chunked, chunked,
            pltpu.VMEM((rows, width), f32),
            pltpu.VMEM((rows, width), f32),
            pltpu.VMEM((chunks, rows, 128), f32),
            pltpu.VMEM((chunks, rows, 128), f32),
            pltpu.VMEM((width, local), bf16),
            pltpu.VMEM((share, 4 * local), bf16),
            pltpu.VMEM((4 * local, width), bf16),
            pltpu.VMEM((share, width // GRAD_PIECES), f32),
            pltpu.VMEM((2, part, width), bf16),
            pltpu.VMEM((2, part, width), bf16),
            pltpu.VMEM((2, part, width), f32),
            pltpu.VMEM((part, width), bf16),
            pltpu.VMEM((part, width), bf16),
            pltpu.VMEM((part, width), bf16),
            dma, dma, dma,
            dma((chunks,)), dma((chunks,)),
            dma((chunks, PIECES)), dma((chunks, PIECES)),
            dma((chunks,)),
            dma((3,)), dma((3,)),
            dma((4, chunks)), dma((4, chunks)),
            dma((GRAD_PIECES,)), dma((GRAD_PIECES,)),
            dma((GRAD_PIECES,)), dma((GRAD_PIECES,)),
            dma((GRAD_PIECES,)),
        ],
        compiler_params=pltpu.CompilerParams(
            collective_id=0, has_side_effects=True, vmem_limit_bytes=67043328),
        cost_estimate=pl.CostEstimate(
            flops=6 * local * width * width, bytes_accessed=2 * width * width, transcendentals=0),
        name="relay",
    )(sample_ids, inputs, stored, weight, norm_gain)


def per_device(inputs, sample_ids, stored, weight, norm_gain):
    batches, tokens, width = inputs.shape
    scale = 1.0 / math.sqrt(lax.axis_size("dp") * batches * tokens)
    outs, summed = relay(scale, inputs, sample_ids, stored, weight, norm_gain)
    return (outs[None], summed[None])


def solution(mesh):
    return jax.shard_map(
        per_device,
        mesh=mesh,
        in_specs=(
            P("dp", None, None),
            P("dp", None),
            P("section", None, "dp", None, None),
            P("section", None, None),
            P("section", None),
        ),
        out_specs=(P("section", "dp", None, None), P("section", "dp", None)),
        check_vma=False,
    )
```

time: 398 us -> 265 us (0.67)
  the two profiles are of different devices: /device:TPU:8 before, /device:TPU:1 now
where the time goes in v2:
time: 265 us
  Pallas kernels  261 us (98%)
  local copies, waits for them, and re-layouts  3.76 us (1%)
    pallas_call x1, Pallas kernels, relay(): pl.pallas_call(functools.partial(relay_kernel, scale), out_shape=(jax.Sha...  261 us

profile of v2, /device:TPU:1, one launch (start us, length us, event | category | flops | bytes accessed | tf_op | source)
XLA Modules:
  0.0 265.2 jit_solution(10292885266700682809)
XLA Ops:
  0.6 260.8 %relay.1 = (bf16[2,128,3072]{2,1,0:T(8,128)(2,1)}, bf16[192,3072]{1,0:T(8,128)(2,1)}) custom-call(s32[1,2]{1,0:T(1,128)} %ids_ref.1, bf16[2,128,3072]{2,1,0:T(8,128)(2,1)} %inputs_hbm.1, bf16[1,2,2,128,3072]{4,3,2,1,0:T(8,128)(2,1)} %stored_hbm.1, bf16[1,3072,3072]{2,1,0:T(8,128)(2,1)} %w_hbm.1, f32[1,3072]{1,0:T(1,128)} %gain_ref.1), custom_call_target="tpu_custom_call" | custom-call | flops 14495514624 | bytes 18874368 | tf_op jit(solution)/shard_map/relay/pallas_call | solution.py:372
  261.4 0.0 copy-start
  261.4 2.7 %copy.9 = bf16[1,2,128,3072]{3,2,1,0:T(8,128)(2,1)} copy(bf16[1,2,128,3072]{3,2,1,0:T(8,128)(2,1)} %bitcast.2) | data formatting | bytes 3145728
  264.2 0.0 copy-done
  264.2 1.0 copy.10
Async XLA Ops:
  261.4 2.8 %copy-start = (bf16[192,3072]{1,0:T(8,128)(2,1)S(1)}, bf16[192,3072]{1,0:T(8,128)(2,1)}, u32[]{:S(2)}) copy-start(bf16[192,3072]{1,0:T(8,128)(2,1)} %get-tuple-element.5) | copy-start | bytes 3538948

commit v3 on v2

--- a/solution.py
+++ b/solution.py
@@ -24,9 +24,9 @@
     scale,
     ids_ref, inputs_hbm, stored_hbm, w_hbm, gain_ref,
     out_hbm, wgrad_hbm,
-    w_v, base_v, keep_v, fin_v, clip_v, normed_v, pre_v, out_v, bin_v, bout_v,
-    acc_v, up_v, mu_v, rs_v,
-    nt_v, ngat_v, ggat_v, tile_v, csend_v, crecv_v, own_v, ysend_v, yrecv_v, res_v,
+    w_v, wt_v, base_v, keep_v, fin_v, clip_v, normed_v, pre_v, out_v, bin_v,
+    up_v, mu_v, rs_v, u_v,
+    nt_v, ngat_v, ggat_v, crecv_v, yrecv_v,
     sem_w, sem_base, sem_keep, fsend, frecv, bsend, brecv, sem_out,
     nsend, nrecv, zsend, zrecv, csend, crecv, ysend, yrecv, sem_res,
 ):
@@ -95,6 +95,39 @@
     pltpu.make_async_copy(stored_hbm.at[0, 1], keep_v, sem_keep).wait()
     pltpu.make_async_copy(w_hbm.at[0], w_v, sem_w).wait()
 
+    @pl.when(has_prev)
+    def _():
+        side = 256
+        line = lax.broadcasted_iota(jnp.int32, (side, side), 0)
+        column = lax.broadcasted_iota(jnp.int32, (side, side), 1)
+        eye = jnp.where(line == column, 1.0, 0.0).astype(bf16)
+
+        def turn(i, carry):
+            cols = pl.ds(pl.multiple_of(i * side, side), side)
+            for j in range(PIECES):
+                part = pl.ds(j * block, block)
+                wt_v[cols, part] = lax.dot_general(
+                    eye, w_v[part, cols], (((1,), (1,)), ((), ())), preferred_element_type=f32).astype(bf16)
+            return carry
+
+        lax.fori_loop(0, width // side, turn, 0)
+        high = gain_ref[...].astype(bf16)
+        low = (gain_ref[...] - high.astype(f32)).astype(bf16)
+        which = lax.broadcasted_iota(jnp.int32, (16, width), 0)
+        pair = jnp.where(which == 0, high.astype(f32), jnp.where(which == 1, low.astype(f32), 0.0)).astype(bf16)
+
+        def weigh(j, carry):
+            cols = pl.ds(pl.multiple_of(j * block, block), block)
+            both = jnp.dot(pair, w_v[:, cols], preferred_element_type=f32)
+            u_v[:, cols] = jnp.broadcast_to(jnp.sum(both, axis=0, keepdims=True), (8, block))
+            return carry
+
+        lax.fori_loop(0, PIECES, weigh, 0)
+
+    @pl.when(s == 0)
+    def _():
+        u_v[...] = jnp.zeros_like(u_v)
+
     def remote(src, dst, send, recv, device):
         return pltpu.make_async_remote_copy(
             src_ref=src, dst_ref=dst, send_sem=send, recv_sem=recv, device_id=device, device_id_type=MESH)
@@ -110,7 +143,7 @@
 
     def bcopy(c, j):
         cols = cols_of(j)
-        return remote(bout_v.at[c, :, cols], bin_v.at[c, :, cols], bsend.at[c, j], brecv.at[c, j], prv)
+        return remote(clip_v.at[c, :, cols], bin_v.at[c, :, cols], bsend.at[c, j], brecv.at[c, j], prv)
 
     def place(c):
         batch = c // per_batch
@@ -165,7 +198,7 @@
         ncopy(3, z_far, dev_far).start()
         ngat_v[:, pl.ds(0, local)] = nt_v[pl.ds(pl.multiple_of(z * share, share), share)]
 
-    def forward(c, carry):
+    def forward(c):
         batch, first, sample, index = place(c)
 
         @pl.when(has_prev)
@@ -199,19 +232,11 @@
 
         lax.fori_loop(0, PIECES, tile, 0)
         pltpu.make_async_copy(out_v.at[c], out_hbm.at[batch, pl.ds(first, rows)], sem_out.at[c]).start()
-        return carry
-
-    lax.fori_loop(0, chunks, forward, 0)
-
-    @pl.when(has_next)
-    def _():
-        share_normed()
-
-    def backward(c, carry):
+
+    def backward(c):
         batch, first, sample, index = place(c)
-        acc_v[...] = jnp.zeros_like(acc_v)
-
-        def tile(j, carry2):
+
+        def piece(j, sums):
             cols = cols_of(j)
 
             @pl.when(has_next)
@@ -226,41 +251,67 @@
             up_v[:, cols] = up
             gp = (slope * up).astype(bf16)
             ggat_v[slot_rows(0, c), cols] = gp
-
-            @pl.when(has_prev)
-            def _():
-                acc_v[...] += lax.dot_general(
-                    gp, w_v[:, cols], (((1,), (1,)), ((), ())), preferred_element_type=f32)
-
-            return carry2
-
-        lax.fori_loop(0, PIECES, tile, 0)
+            wide_gp = gp.astype(f32)
+            return (
+                sums[0] + jnp.sum(wide_gp * u_v[0:1, cols], axis=-1, keepdims=True),
+                sums[1] + jnp.sum(wide_gp * v, axis=-1, keepdims=True),
+            )
+
+        zero = jnp.zeros((rows, 1), f32)
+        sums = lax.fori_loop(0, PIECES, piece, (zero, zero))
         to_up(c).start()
         to_down(c).start()
 
         @pl.when(has_prev)
         def _():
+            m1 = sums[0] * (1.0 / width)
+            m2 = sums[1] * (1.0 / width)
             mu = mu_v[c][:, :1]
             rs = rs_v[c][:, :1]
-            x = base_v[index, pl.ds(first, rows), :].astype(f32) + fin_v[c].astype(f32)
-            xhat = (x - mu) * rs
-            dx = acc_v[...] * gain_ref[...]
-            m1 = jnp.mean(dx, axis=-1, keepdims=True)
-            m2 = jnp.mean(dx * xhat, axis=-1, keepdims=True)
-            bout_v[c] = (up_v[...] + rs * (dx - m1 - xhat * m2)).astype(bf16)
-            for j in range(PIECES):
+
+            @pl.when(has_next)
+            def _():
+                fwhole(c).wait_send()
+
+            def tile(j, carry2):
+                cols = cols_of(j)
+                gn = jnp.dot(ggat_v[slot_rows(0, c)], wt_v[:, cols], preferred_element_type=f32)
+                state = base_v[index, pl.ds(first, rows), cols].astype(f32) + fin_v[c, :, cols].astype(f32)
+                xhat = (state - mu) * rs
+                clip_v[c, :, cols] = (
+                    up_v[:, cols] + rs * (gn * gain_ref[:, cols] - m1 - xhat * m2)
+                ).astype(bf16)
                 bcopy(c, j).start()
+                return carry2
+
+            lax.fori_loop(0, PIECES, tile, 0)
 
         @pl.when(c >= 1)
         def _():
             pass_on(c - 1)
 
+    ahead = jnp.minimum(chunks, ((last - s) * 7 + 1) // 2)
+    early = ahead == chunks
+
+    def step(t, carry):
+        @pl.when(t < chunks)
+        def _():
+            forward(t)
+
+        @pl.when(jnp.logical_and(t == chunks - 1, early))
+        def _():
+            share_normed()
+
+        @pl.when(t >= ahead)
+        def _():
+            backward(t - ahead)
+
         return carry
 
-    lax.fori_loop(0, chunks, backward, 0)
+    lax.fori_loop(0, chunks + ahead, step, 0)
     pass_on(chunks - 1)
 
-    @pl.when(s == last)
+    @pl.when(jnp.logical_not(early))
     def _():
         share_normed()
 
@@ -280,35 +331,47 @@
     def lanes_of(q):
         return pl.ds(pl.multiple_of(q * wide, wide), wide)
 
-    def core_copy(q):
+    def held(place_of):
+        return pl.ds(place_of * part, part)
+
+    def core_copy(q, y):
         lanes = lanes_of(q)
-        return remote(csend_v.at[:, :, lanes], crecv_v.at[:, :, lanes], csend.at[q], crecv.at[q], dev_core)
+        return remote(w_v.at[held(y), lanes], crecv_v.at[y, :, lanes], csend.at[q, y], crecv.at[q, y], dev_core)
 
     def row_copy(q):
         lanes = lanes_of(q)
-        return remote(ysend_v.at[:, lanes], yrecv_v.at[:, lanes], ysend.at[q], yrecv.at[q], dev_row)
+        return remote(w_v.at[held(4), lanes], yrecv_v.at[:, lanes], ysend.at[q], yrecv.at[q], dev_row)
 
     def res_copy(q):
         lanes = lanes_of(q)
-        return pltpu.make_async_copy(res_v.at[:, lanes], wgrad_hbm.at[:, lanes], sem_res.at[q])
+        return pltpu.make_async_copy(w_v.at[held(5), lanes], wgrad_hbm.at[:, lanes], sem_res.at[q])
+
+    def band(y, whose):
+        return pl.ds(pl.multiple_of(y * 2 * part + whose * part, part), part)
+
+    def own_rows(y):
+        return pl.ds(pl.multiple_of((2 + y) * part, part), part)
 
     def product(q, carry):
         @pl.when(q < GRAD_PIECES)
         def _():
             lanes = lanes_of(q)
-            tile_v[...] = jnp.dot(ngat_v[...], ggat_v[:, lanes], preferred_element_type=f32)
             for y in range(2):
-                mine = pl.ds(pl.multiple_of(y * 2 * part + core * part, part), part)
-                other = pl.ds(pl.multiple_of(y * 2 * part + (1 - core) * part, part), part)
-                csend_v[y, :, lanes] = tile_v[other, :].astype(bf16)
-                own_v[y, :, lanes] = tile_v[mine, :]
-            core_copy(q).start()
+                w_v[held(y), lanes] = jnp.dot(
+                    ngat_v[band(y, 1 - core), :], ggat_v[:, lanes], preferred_element_type=f32).astype(bf16)
+                core_copy(q, y).start()
+            for y in range(2):
+                w_v[held(2 + y), lanes] = jnp.dot(
+                    ngat_v[band(y, core), :], ggat_v[:, lanes], preferred_element_type=f32).astype(bf16)
 
         @pl.when(q >= 1)
         def _():
             lanes = lanes_of(q - 1)
-            core_copy(q - 1).wait_recv()
-            ysend_v[:, lanes] = (own_v[1 - row, :, lanes] + crecv_v[1 - row, :, lanes].astype(f32)).astype(bf16)
+            for y in range(2):
+                core_copy(q - 1, y).wait_recv()
+            w_v[held(4), lanes] = (
+                w_v[own_rows(1 - row), lanes].astype(f32) + crecv_v[1 - row, :, lanes].astype(f32)
+            ).astype(bf16)
             row_copy(q - 1).start()
 
         return carry
@@ -318,8 +381,9 @@
     def total(q, carry):
         lanes = lanes_of(q)
         row_copy(q).wait_recv()
-        res_v[:, lanes] = (
-            own_v[row, :, lanes] + crecv_v[row, :, lanes].astype(f32) + yrecv_v[:, lanes].astype(f32)
+        w_v[held(5), lanes] = (
+            w_v[own_rows(row), lanes].astype(f32) + crecv_v[row, :, lanes].astype(f32)
+            + yrecv_v[:, lanes].astype(f32)
         ).astype(bf16)
         res_copy(q).start()
         return carry
@@ -334,7 +398,7 @@
         pass_up(c).wait_send()
         pass_down(c).wait_send()
 
-        @pl.when(has_next)
+        @pl.when(s == 0)
         def _():
             fwhole(c).wait_send()
 
@@ -348,7 +412,8 @@
     lax.fori_loop(0, chunks, finish, 0)
 
     def finish_grad(q, carry):
-        core_copy(q).wait_send()
+        for y in range(2):
+            core_copy(q, y).wait_send()
         row_copy(q).wait_send()
         res_copy(q).wait()
         return carry
@@ -382,24 +447,20 @@
         out_specs=(any_spec, any_spec),
         scratch_shapes=[
             pltpu.VMEM((width, width), bf16),
+            pltpu.VMEM((width, width), bf16),
             pltpu.VMEM(inputs.shape, bf16),
             pltpu.VMEM(inputs.shape, bf16),
             chunked, chunked, chunked,
             pltpu.VMEM((chunks, rows, width), f32),
-            chunked, chunked, chunked,
-            pltpu.VMEM((rows, width), f32),
+            chunked, chunked,
             pltpu.VMEM((rows, width), f32),
             pltpu.VMEM((chunks, rows, 128), f32),
             pltpu.VMEM((chunks, rows, 128), f32),
+            pltpu.VMEM((8, width), f32),
             pltpu.VMEM((width, local), bf16),
             pltpu.VMEM((share, 4 * local), bf16),
             pltpu.VMEM((4 * local, width), bf16),
-            pltpu.VMEM((share, width // GRAD_PIECES), f32),
             pltpu.VMEM((2, part, width), bf16),
-            pltpu.VMEM((2, part, width), bf16),
-            pltpu.VMEM((2, part, width), f32),
-            pltpu.VMEM((part, width), bf16),
-            pltpu.VMEM((part, width), bf16),
             pltpu.VMEM((part, width), bf16),
             dma, dma, dma,
             dma((chunks,)), dma((chunks,)),
@@ -407,7 +468,7 @@
             dma((chunks,)),
             dma((3,)), dma((3,)),
             dma((4, chunks)), dma((4, chunks)),
-            dma((GRAD_PIECES,)), dma((GRAD_PIECES,)),
+            dma((GRAD_PIECES, 2)), dma((GRAD_PIECES, 2)),
             dma((GRAD_PIECES,)), dma((GRAD_PIECES,)),
             dma((GRAD_PIECES,)),
         ],

time: 265 us -> 239 us (0.902)
  the two profiles are of different devices: /device:TPU:1 before, /device:TPU:0 now
where the time goes in v3:
time: 239 us; the launch traced here: 238 us
  Pallas kernels  234 us (98%)
  local copies, waits for them, and re-layouts  3.76 us (2%)
    pallas_call x1, Pallas kernels, relay(): pl.pallas_call(functools.partial(relay_kernel, scale), out_shape=(jax.Sha...  234 us

profile of v3, /device:TPU:0, one launch (start us, length us, event | category | flops | bytes accessed | tf_op | source)
XLA Modules:
  0.0 238.3 jit_solution(9295724615549520106)
XLA Ops:
  0.6 233.9 %relay.1 = (bf16[2,128,3072]{2,1,0:T(8,128)(2,1)}, bf16[192,3072]{1,0:T(8,128)(2,1)}) custom-call(s32[1,2]{1,0:T(1,128)} %ids_ref.1, bf16[2,128,3072]{2,1,0:T(8,128)(2,1)} %inputs_hbm.1, bf16[1,2,2,128,3072]{4,3,2,1,0:T(8,128)(2,1)} %stored_hbm.1, bf16[1,3072,3072]{2,1,0:T(8,128)(2,1)} %w_hbm.1, f32[1,3072]{1,0:T(1,128)} %gain_ref.1), custom_call_target="tpu_custom_call" | custom-call | flops 14495514624 | bytes 18874368 | tf_op jit(solution)/shard_map/relay/pallas_call | solution.py:437
  234.6 0.0 copy-start
  234.6 2.7 %copy.9 = bf16[1,2,128,3072]{3,2,1,0:T(8,128)(2,1)} copy(bf16[1,2,128,3072]{3,2,1,0:T(8,128)(2,1)} %bitcast.2) | data formatting | bytes 3145728
  237.3 0.0 copy-done
  237.3 1.0 copy.10
Async XLA Ops:
  234.6 2.8 %copy-start = (bf16[192,3072]{1,0:T(8,128)(2,1)S(1)}, bf16[192,3072]{1,0:T(8,128)(2,1)}, u32[]{:S(2)}) copy-start(bf16[192,3072]{1,0:T(8,128)(2,1)} %get-tuple-element.5) | copy-start | bytes 3538948

commit v4 on v3

--- a/solution.py
+++ b/solution.py
@@ -25,7 +25,7 @@
     ids_ref, inputs_hbm, stored_hbm, w_hbm, gain_ref,
     out_hbm, wgrad_hbm,
     w_v, wt_v, base_v, keep_v, fin_v, clip_v, normed_v, pre_v, out_v, bin_v,
-    up_v, mu_v, rs_v, u_v,
+    mu_v, rs_v, u_v,
     nt_v, ngat_v, ggat_v, crecv_v, yrecv_v,
     sem_w, sem_base, sem_keep, fsend, frecv, bsend, brecv, sem_out,
     nsend, nrecv, zsend, zrecv, csend, crecv, ysend, yrecv, sem_res,
@@ -57,7 +57,11 @@
     dev_core = {"dp": d + 1 - 2 * core}
     dev_row = {"dp": z * 4 + (rest + 2) % 4}
 
-    pltpu.make_async_copy(w_hbm.at[0], w_v, sem_w).start()
+    late = s < last - 2
+
+    def w_copy(j):
+        cols = pl.ds(pl.multiple_of(j * block, block), block)
+        return pltpu.make_async_copy(w_hbm.at[0, :, cols], w_v.at[:, cols], sem_w.at[j])
 
     @pl.when(s == 0)
     def _():
@@ -67,6 +71,8 @@
     def _():
         pltpu.make_async_copy(stored_hbm.at[0, 0], base_v, sem_base).start()
 
+    for j in range(PIECES):
+        w_copy(j).start()
     pltpu.make_async_copy(stored_hbm.at[0, 1], keep_v, sem_keep).start()
 
     barrier = pltpu.get_barrier_semaphore()
@@ -87,16 +93,8 @@
     def _():
         fin_v[...] = jnp.zeros_like(fin_v)
 
-    @pl.when(s == last)
-    def _():
-        bin_v[...] = jnp.zeros_like(bin_v)
-
     pltpu.make_async_copy(inputs_hbm, base_v, sem_base).wait()
-    pltpu.make_async_copy(stored_hbm.at[0, 1], keep_v, sem_keep).wait()
-    pltpu.make_async_copy(w_hbm.at[0], w_v, sem_w).wait()
-
-    @pl.when(has_prev)
-    def _():
+    def prepare():
         side = 256
         line = lax.broadcasted_iota(jnp.int32, (side, side), 0)
         column = lax.broadcasted_iota(jnp.int32, (side, side), 1)
@@ -128,6 +126,14 @@
     def _():
         u_v[...] = jnp.zeros_like(u_v)
 
+    @pl.when(jnp.logical_not(late))
+    def _():
+        for j in range(PIECES):
+            w_copy(j).wait()
+        prepare()
+
+    pltpu.make_async_copy(stored_hbm.at[0, 1], keep_v, sem_keep).wait()
+
     def remote(src, dst, send, recv, device):
         return pltpu.make_async_remote_copy(
             src_ref=src, dst_ref=dst, send_sem=send, recv_sem=recv, device_id=device, device_id_type=MESH)
@@ -155,8 +161,12 @@
     share = width // 4
     half = width // 2
 
-    def slot_rows(slot, c):
-        return pl.ds(pl.multiple_of(slot * local + c * rows, rows), rows)
+    def slot_rows(slot, c, n=1):
+        return pl.ds(pl.multiple_of(slot * local + c * rows, rows), n * rows)
+
+    def out_copy(c):
+        batch, first, sample, index = place(c)
+        return pltpu.make_async_copy(out_v.at[c], out_hbm.at[batch, pl.ds(first, rows)], sem_out.at[c])
 
     def to_up(c):
         return remote(ggat_v.at[slot_rows(0, c)], ggat_v.at[slot_rows(1, c)], zsend.at[0, c], zrecv.at[0, c], dev_up)
@@ -198,120 +208,170 @@
         ncopy(3, z_far, dev_far).start()
         ngat_v[:, pl.ds(0, local)] = nt_v[pl.ds(pl.multiple_of(z * share, share), share)]
 
-    def forward(c):
+    def several(ref, c, n, cols=None):
+        if cols is None:
+            return ref[pl.ds(c, n)].reshape(n * rows, ref.shape[-1])
+        return ref[pl.ds(c, n), :, cols].reshape(n * rows, cols.size)
+
+    def keep(ref, c, n, value, cols=None):
+        if cols is None:
+            ref[pl.ds(c, n)] = value.reshape(n, rows, value.shape[-1])
+        else:
+            ref[pl.ds(c, n), :, cols] = value.reshape(n, rows, cols.size)
+
+    def state_of(c, n, cols=None):
         batch, first, sample, index = place(c)
-
-        @pl.when(has_prev)
-        def _():
-            fwhole(c).wait_recv()
-
-        x = base_v[index, pl.ds(first, rows), :].astype(f32) + fin_v[c].astype(f32)
+        if cols is None:
+            return base_v[index, pl.ds(first, n * rows), :].astype(f32) + several(fin_v, c, n).astype(f32)
+        return base_v[index, pl.ds(first, n * rows), cols].astype(f32) + several(fin_v, c, n, cols).astype(f32)
+
+    def forward(c, n, final):
+        batch, first, sample, index = place(c)
+        if final:
+            for i in range(n):
+                fwhole(c + i).wait_recv()
+        else:
+            @pl.when(has_prev)
+            def _():
+                fwhole(c).wait_recv()
+
+        x = state_of(c, n)
         mu = jnp.mean(x, axis=-1, keepdims=True)
         xc = x - mu
         var = jnp.mean(xc * xc, axis=-1, keepdims=True)
         rs = lax.rsqrt(var + epsilon)
-        normed_v[c] = (xc * rs * gain_ref[...]).astype(bf16)
-        mu_v[c] = jnp.broadcast_to(mu, (rows, 128))
-        rs_v[c] = jnp.broadcast_to(rs, (rows, 128))
+        keep(normed_v, c, n, (xc * rs * gain_ref[...]).astype(bf16))
+        keep(mu_v, c, n, jnp.broadcast_to(mu, (n * rows, 128)))
+        keep(rs_v, c, n, jnp.broadcast_to(rs, (n * rows, 128)))
 
         def tile(j, carry2):
             cols = cols_of(j)
-            v = jnp.dot(normed_v[c], w_v[:, cols], preferred_element_type=f32)
-            pre_v[c, :, cols] = v
-            state = base_v[index, pl.ds(first, rows), cols].astype(f32) + fin_v[c, :, cols].astype(f32)
-            res = state + v * (0.5 + 0.5 * lax.erf(v * rsqrt2))
-            out_v[c, :, cols] = res.astype(bf16)
-            kept = keep_v[sample, pl.ds(first, rows), cols].astype(f32)
-            clip_v[c, :, cols] = jnp.clip(res - kept, -delta_bound, delta_bound).astype(bf16)
-
-            @pl.when(has_next)
-            def _():
+            if not final:
+                @pl.when(jnp.logical_and(c == 0, late))
+                def _():
+                    w_copy(j).wait()
+
+            v = jnp.dot(several(normed_v, c, n), w_v[:, cols], preferred_element_type=f32)
+            keep(pre_v, c, n, v, cols)
+            res = state_of(c, n, cols) + v * (0.5 + 0.5 * lax.erf(v * rsqrt2))
+            keep(out_v, c, n, res.astype(bf16), cols)
+            if not final:
+                kept = keep_v[sample, pl.ds(first, rows), cols].astype(f32)
+                clip_v[c, :, cols] = jnp.clip(res - kept, -delta_bound, delta_bound).astype(bf16)
                 fcopy(c, cols).start()
-
             return carry2
 
         lax.fori_loop(0, PIECES, tile, 0)
-        pltpu.make_async_copy(out_v.at[c], out_hbm.at[batch, pl.ds(first, rows)], sem_out.at[c]).start()
-
-    def backward(c):
-        batch, first, sample, index = place(c)
-
+        for i in range(n):
+            out_copy(c + i).start()
+
+    def backward(c, n, final):
         def piece(j, sums):
             cols = cols_of(j)
-
-            @pl.when(has_next)
-            def _():
+            if not final:
                 bcopy(c, j).wait_recv()
-
-            v = pre_v[c, :, cols]
+            v = several(pre_v, c, n, cols)
             cdf = 0.5 + 0.5 * lax.erf(v * rsqrt2)
             slope = cdf + v * (jnp.exp(-0.5 * v * v) * rsqrt2pi)
-            state = base_v[index, pl.ds(first, rows), cols].astype(f32) + fin_v[c, :, cols].astype(f32)
-            up = jnp.where(s == last, (state + v * cdf) * scale, bin_v[c, :, cols].astype(f32))
-            up_v[:, cols] = up
+            if final:
+                up = (state_of(c, n, cols) + v * cdf) * scale
+            else:
+                up = several(bin_v, c, n, cols).astype(f32)
             gp = (slope * up).astype(bf16)
-            ggat_v[slot_rows(0, c), cols] = gp
+            ggat_v[slot_rows(0, c, n), cols] = gp
             wide_gp = gp.astype(f32)
             return (
                 sums[0] + jnp.sum(wide_gp * u_v[0:1, cols], axis=-1, keepdims=True),
                 sums[1] + jnp.sum(wide_gp * v, axis=-1, keepdims=True),
             )
 
-        zero = jnp.zeros((rows, 1), f32)
+        zero = jnp.zeros((n * rows, 1), f32)
         sums = lax.fori_loop(0, PIECES, piece, (zero, zero))
-        to_up(c).start()
-        to_down(c).start()
-
-        @pl.when(has_prev)
-        def _():
+        for i in range(n):
+            to_up(c + i).start()
+            to_down(c + i).start()
+
+        def pull():
             m1 = sums[0] * (1.0 / width)
             m2 = sums[1] * (1.0 / width)
-            mu = mu_v[c][:, :1]
-            rs = rs_v[c][:, :1]
-
-            @pl.when(has_next)
-            def _():
+            mu = several(mu_v, c, n)[:, :1]
+            rs = several(rs_v, c, n)[:, :1]
+            if not final:
                 fwhole(c).wait_send()
 
             def tile(j, carry2):
                 cols = cols_of(j)
-                gn = jnp.dot(ggat_v[slot_rows(0, c)], wt_v[:, cols], preferred_element_type=f32)
-                state = base_v[index, pl.ds(first, rows), cols].astype(f32) + fin_v[c, :, cols].astype(f32)
+                gn = jnp.dot(ggat_v[slot_rows(0, c, n)], wt_v[:, cols], preferred_element_type=f32)
+                state = state_of(c, n, cols)
                 xhat = (state - mu) * rs
-                clip_v[c, :, cols] = (
-                    up_v[:, cols] + rs * (gn * gain_ref[:, cols] - m1 - xhat * m2)
-                ).astype(bf16)
+                if final:
+                    v = several(pre_v, c, n, cols)
+                    up = (state + v * (0.5 + 0.5 * lax.erf(v * rsqrt2))) * scale
+                else:
+                    up = several(bin_v, c, n, cols).astype(f32)
+                sent = up + rs * (gn * gain_ref[:, cols] - m1 - xhat * m2)
+                keep(clip_v, c, n, sent.astype(bf16), cols)
                 bcopy(c, j).start()
                 return carry2
 
             lax.fori_loop(0, PIECES, tile, 0)
-
-        @pl.when(c >= 1)
-        def _():
-            pass_on(c - 1)
-
-    ahead = jnp.minimum(chunks, ((last - s) * 7 + 1) // 2)
-    early = ahead == chunks
+            for i in range(1, n):
+                for j in range(PIECES):
+                    bcopy(c + i, j).start()
+
+        if final:
+            pull()
+        else:
+            pl.when(has_prev)(pull)
+
+    ahead = jnp.where(s == last - 1, chunks - 2, chunks)
 
     def step(t, carry):
         @pl.when(t < chunks)
         def _():
-            forward(t)
-
-        @pl.when(jnp.logical_and(t == chunks - 1, early))
+            forward(t, 1, False)
+
+        @pl.when(jnp.logical_and(t == chunks - 1, late))
         def _():
             share_normed()
 
+            @pl.when(has_prev)
+            def _():
+                prepare()
+
+        @pl.when(t > ahead)
+        def _():
+            pass_on(t - ahead - 1)
+
         @pl.when(t >= ahead)
         def _():
-            backward(t - ahead)
-
-        return carry
-
-    lax.fori_loop(0, chunks + ahead, step, 0)
+            backward(t - ahead, 1, False)
+
+        return carry
+
+    def pair_step(t, carry):
+        forward(2 * t, 2, True)
+
+        @pl.when(t > 0)
+        def _():
+            pass_on(2 * t - 2)
+            pass_on(2 * t - 1)
+
+        backward(2 * t, 2, True)
+        return carry
+
+    @pl.when(has_next)
+    def _():
+        lax.fori_loop(0, chunks + ahead, step, 0)
+
+    @pl.when(s == last)
+    def _():
+        lax.fori_loop(0, chunks // 2, pair_step, 0)
+        pass_on(chunks - 2)
+
     pass_on(chunks - 1)
 
-    @pl.when(jnp.logical_not(early))
+    @pl.when(jnp.logical_not(late))
     def _():
         share_normed()
 
@@ -391,8 +451,7 @@
     lax.fori_loop(0, GRAD_PIECES, total, 0)
 
     def finish(c, carry):
-        batch, first, sample, index = place(c)
-        pltpu.make_async_copy(out_v.at[c], out_hbm.at[batch, pl.ds(first, rows)], sem_out.at[c]).wait()
+        out_copy(c).wait()
         to_up(c).wait_send()
         to_down(c).wait_send()
         pass_up(c).wait_send()
@@ -453,7 +512,6 @@
             chunked, chunked, chunked,
             pltpu.VMEM((chunks, rows, width), f32),
             chunked, chunked,
-            pltpu.VMEM((rows, width), f32),
             pltpu.VMEM((chunks, rows, 128), f32),
             pltpu.VMEM((chunks, rows, 128), f32),
             pltpu.VMEM((8, width), f32),
@@ -462,7 +520,7 @@
             pltpu.VMEM((4 * local, width), bf16),
             pltpu.VMEM((2, part, width), bf16),
             pltpu.VMEM((part, width), bf16),
-            dma, dma, dma,
+            dma((PIECES,)), dma, dma,
             dma((chunks,)), dma((chunks,)),
             dma((chunks, PIECES)), dma((chunks, PIECES)),
             dma((chunks,)),

time: 239 us -> 241 us (level)
  the two profiles are of different devices: /device:TPU:0 before, /device:TPU:32 now
where the time goes in v4:
time: 241 us
  Pallas kernels  237 us (98%)
  local copies, waits for them, and re-layouts  3.76 us (2%)
    pallas_call x1, Pallas kernels, relay(): pl.pallas_call(functools.partial(relay_kernel, scale), out_shape=(jax.Sha...  237 us

profile of v4, /device:TPU:32, one launch (start us, length us, event | category | flops | bytes accessed | tf_op | source)
XLA Modules:
  0.0 241.2 jit_solution(2044348754886527504)
XLA Ops:
  0.6 236.8 %relay.1 = (bf16[2,128,3072]{2,1,0:T(8,128)(2,1)}, bf16[192,3072]{1,0:T(8,128)(2,1)}) custom-call(s32[1,2]{1,0:T(1,128)} %ids_ref.1, bf16[2,128,3072]{2,1,0:T(8,128)(2,1)} %inputs_hbm.1, bf16[1,2,2,128,3072]{4,3,2,1,0:T(8,128)(2,1)} %stored_hbm.1, bf16[1,3072,3072]{2,1,0:T(8,128)(2,1)} %w_hbm.1, f32[1,3072]{1,0:T(1,128)} %gain_ref.1), custom_call_target="tpu_custom_call" | custom-call | flops 14495514624 | bytes 18874368 | tf_op jit(solution)/shard_map/relay/pallas_call | solution.py:496
  237.4 0.0 copy-start
  237.4 2.7 %copy.9 = bf16[1,2,128,3072]{3,2,1,0:T(8,128)(2,1)} copy(bf16[1,2,128,3072]{3,2,1,0:T(8,128)(2,1)} %bitcast.2) | data formatting | bytes 3145728
  240.2 0.0 copy-done
  240.2 1.0 copy.10
Async XLA Ops:
  237.4 2.8 %copy-start = (bf16[192,3072]{1,0:T(8,128)(2,1)S(1)}, bf16[192,3072]{1,0:T(8,128)(2,1)}, u32[]{:S(2)}) copy-start(bf16[192,3072]{1,0:T(8,128)(2,1)} %get-tuple-element.5) | copy-start | bytes 3538948

commit v5 on v4

--- a/solution.py
+++ b/solution.py
@@ -12,7 +12,7 @@
 delta_bound = 2.0
 CHUNK = 32
 PIECES = 4
-GRAD_PIECES = 6
+Z_UNITS = 7
 MESH = pl.DeviceIdType.MESH
 f32 = jnp.float32
 bf16 = jnp.bfloat16
@@ -26,9 +26,10 @@
     out_hbm, wgrad_hbm,
     w_v, wt_v, base_v, keep_v, fin_v, clip_v, normed_v, pre_v, out_v, bin_v,
     mu_v, rs_v, u_v,
-    nt_v, ngat_v, ggat_v, crecv_v, yrecv_v,
+    nt_v, ngat_v, nrow_v, gown_v, gz_v, gy_v,
     sem_w, sem_base, sem_keep, fsend, frecv, bsend, brecv, sem_out,
-    nsend, nrecv, zsend, zrecv, csend, crecv, ysend, yrecv, sem_res,
+    nsend, nrecv, zsend, zrecv, gsend, grecv, csend, crecv, ysend, yrecv,
+    csend2, crecv2, zsend2, zrecv2, sem_res, ready,
 ):
     s = lax.axis_index("section")
     sections = lax.axis_size("section")
@@ -159,54 +160,50 @@
         return batch, first, sample, index
 
     share = width // 4
-    half = width // 2
-
-    def slot_rows(slot, c, n=1):
-        return pl.ds(pl.multiple_of(slot * local + c * rows, rows), n * rows)
+    part = share // 4
+    unit = width // 12
+    split = unit * Z_UNITS
+    low_lanes = pl.ds(0, split)
+    high_lanes = pl.ds(split, width - split)
+
+    def chunk_rows(c, n=1):
+        return pl.ds(pl.multiple_of(c * rows, rows), n * rows)
 
     def out_copy(c):
         batch, first, sample, index = place(c)
         return pltpu.make_async_copy(out_v.at[c], out_hbm.at[batch, pl.ds(first, rows)], sem_out.at[c])
 
-    def to_up(c):
-        return remote(ggat_v.at[slot_rows(0, c)], ggat_v.at[slot_rows(1, c)], zsend.at[0, c], zrecv.at[0, c], dev_up)
-
-    def to_down(c):
-        return remote(ggat_v.at[slot_rows(0, c)], ggat_v.at[slot_rows(2, c)], zsend.at[1, c], zrecv.at[1, c], dev_down)
-
-    def pass_up(c):
-        lanes = pl.ds(0, half)
-        return remote(ggat_v.at[slot_rows(1, c), lanes], ggat_v.at[slot_rows(3, c), lanes],
-                      zsend.at[2, c], zrecv.at[2, c], dev_up)
-
-    def pass_down(c):
-        lanes = pl.ds(half, half)
-        return remote(ggat_v.at[slot_rows(2, c), lanes], ggat_v.at[slot_rows(3, c), lanes],
-                      zsend.at[3, c], zrecv.at[3, c], dev_down)
-
-    def pass_on(c):
-        to_up(c).wait_recv()
-        pass_up(c).start()
-        to_down(c).wait_recv()
-        pass_down(c).start()
-
-    def ncopy(slot, z_to, device):
-        return remote(nt_v.at[pl.ds(pl.multiple_of(z_to * share, share), share)],
-                      ngat_v.at[:, pl.ds(slot * local, local)], nsend.at[slot - 1], nrecv.at[slot - 1], device)
+    circle = ((0, z_up, dev_up), (1, z_down, dev_down), (2, z_far, dev_far))
+
+    def z_copy(c, slot):
+        return remote(gown_v.at[chunk_rows(c), low_lanes],
+                      gz_v.at[pl.ds(pl.multiple_of(slot * local + c * rows, rows), rows)],
+                      zsend.at[slot, c], zrecv.at[slot, c], circle[slot][2])
+
+    def g_copy(c):
+        return remote(gown_v.at[chunk_rows(c), high_lanes], gy_v.at[chunk_rows(c)], gsend.at[c], grecv.at[c], dev_row)
+
+    def ncopy(slot):
+        return remote(nt_v.at[circle[slot][1]],
+                      ngat_v.at[:, pl.ds((slot + 1) * local, local)], nsend.at[slot], nrecv.at[slot], circle[slot][2])
+
+    def nrow_copy():
+        return remote(nt_v.at[:, pl.ds(pl.multiple_of((1 - row) * 2 * part, 2 * part), 2 * part)], nrow_v,
+                      nsend.at[3], nrecv.at[3], dev_row)
 
     def share_normed():
-        step = 256
+        step = share // 3
         def turn(i, carry):
             cols = pl.ds(pl.multiple_of(i * step, step), step)
             for b in range(batches):
                 values = normed_v[pl.ds(b * per_batch, per_batch), :, cols].reshape(tokens, step)
-                nt_v[cols, pl.ds(b * tokens, tokens)] = values.T
+                nt_v[i // 3, pl.ds(pl.multiple_of((i % 3) * step, step), step), pl.ds(b * tokens, tokens)] = values.T
             return carry
         lax.fori_loop(0, width // step, turn, 0)
-        ncopy(1, z_up, dev_up).start()
-        ncopy(2, z_down, dev_down).start()
-        ncopy(3, z_far, dev_far).start()
-        ngat_v[:, pl.ds(0, local)] = nt_v[pl.ds(pl.multiple_of(z * share, share), share)]
+        for slot in range(3):
+            ncopy(slot).start()
+        nrow_copy().start()
+        ngat_v[:, pl.ds(0, local)] = nt_v[z]
 
     def several(ref, c, n, cols=None):
         if cols is None:
@@ -278,7 +275,7 @@
             else:
                 up = several(bin_v, c, n, cols).astype(f32)
             gp = (slope * up).astype(bf16)
-            ggat_v[slot_rows(0, c, n), cols] = gp
+            gown_v[chunk_rows(c, n), cols] = gp
             wide_gp = gp.astype(f32)
             return (
                 sums[0] + jnp.sum(wide_gp * u_v[0:1, cols], axis=-1, keepdims=True),
@@ -288,8 +285,13 @@
         zero = jnp.zeros((n * rows, 1), f32)
         sums = lax.fori_loop(0, PIECES, piece, (zero, zero))
         for i in range(n):
-            to_up(c + i).start()
-            to_down(c + i).start()
+            for slot in range(3):
+                z_copy(c + i, slot).start()
+
+        if not final:
+            @pl.when(s == 0)
+            def _():
+                g_copy(c).start()
 
         def pull():
             m1 = sums[0] * (1.0 / width)
@@ -301,7 +303,7 @@
 
             def tile(j, carry2):
                 cols = cols_of(j)
-                gn = jnp.dot(ggat_v[slot_rows(0, c, n)], wt_v[:, cols], preferred_element_type=f32)
+                gn = jnp.dot(gown_v[chunk_rows(c, n)], wt_v[:, cols], preferred_element_type=f32)
                 state = state_of(c, n, cols)
                 xhat = (state - mu) * rs
                 if final:
@@ -339,10 +341,6 @@
             def _():
                 prepare()
 
-        @pl.when(t > ahead)
-        def _():
-            pass_on(t - ahead - 1)
-
         @pl.when(t >= ahead)
         def _():
             backward(t - ahead, 1, False)
@@ -352,11 +350,6 @@
     def pair_step(t, carry):
         forward(2 * t, 2, True)
 
-        @pl.when(t > 0)
-        def _():
-            pass_on(2 * t - 2)
-            pass_on(2 * t - 1)
-
         backward(2 * t, 2, True)
         return carry
 
@@ -367,95 +360,162 @@
     @pl.when(s == last)
     def _():
         lax.fori_loop(0, chunks // 2, pair_step, 0)
-        pass_on(chunks - 2)
-
-    pass_on(chunks - 1)
+
+    for peer in (dev_up, dev_down, dev_far, dev_core, dev_row):
+        pl.semaphore_signal(ready, inc=1, device_id=peer, device_id_type=MESH)
+
+    def start_rows(c, carry):
+        g_copy(c).start()
+        return carry
+
+    @pl.when(has_prev)
+    def _():
+        lax.fori_loop(0, chunks, start_rows, 0)
 
     @pl.when(jnp.logical_not(late))
     def _():
         share_normed()
 
-    def arrived(c, carry):
-        pass_up(c).wait_recv()
-        pass_down(c).wait_recv()
-        return carry
-
-    ncopy(1, z_up, dev_up).wait_recv()
-    ncopy(2, z_down, dev_down).wait_recv()
-    ncopy(3, z_far, dev_far).wait_recv()
-    lax.fori_loop(0, chunks, arrived, 0)
-
-    part = share // 4
-    wide = width // GRAD_PIECES
+    def band(place_of, lanes, count=1):
+        return (pl.ds(place_of * part, count * part), lanes)
 
     def lanes_of(q):
-        return pl.ds(pl.multiple_of(q * wide, wide), wide)
-
-    def held(place_of):
-        return pl.ds(place_of * part, part)
+        return pl.ds(pl.multiple_of(q * unit, unit), unit)
 
     def core_copy(q, y):
         lanes = lanes_of(q)
-        return remote(w_v.at[held(y), lanes], crecv_v.at[y, :, lanes], csend.at[q, y], crecv.at[q, y], dev_core)
+        return remote(w_v.at[band(y, lanes)], wt_v.at[band(y, lanes)], csend.at[q, y], crecv.at[q, y], dev_core)
 
     def row_copy(q):
         lanes = lanes_of(q)
-        return remote(w_v.at[held(4), lanes], yrecv_v.at[:, lanes], ysend.at[q], yrecv.at[q], dev_row)
+        return remote(w_v.at[band(4, lanes)], wt_v.at[band(2, lanes)], ysend.at[q], yrecv.at[q], dev_row)
+
+    def core_copy2(q):
+        lanes = lanes_of(q)
+        return remote(w_v.at[band(6, lanes, 4)], wt_v.at[band(3, lanes, 4)], csend2.at[q], crecv2.at[q], dev_core)
+
+    def sum_rows(z_of):
+        return pl.ds(pl.multiple_of((10 + z_of) * part, part), part)
+
+    def z_copy2(q, slot):
+        lanes = lanes_of(q)
+        return remote(w_v.at[sum_rows(circle[slot][1]), lanes], wt_v.at[band(7 + slot, lanes)],
+                      zsend2.at[slot, q], zrecv2.at[slot, q], circle[slot][2])
 
     def res_copy(q):
         lanes = lanes_of(q)
-        return pltpu.make_async_copy(w_v.at[held(5), lanes], wgrad_hbm.at[:, lanes], sem_res.at[q])
-
-    def band(y, whose):
-        return pl.ds(pl.multiple_of(y * 2 * part + whose * part, part), part)
-
-    def own_rows(y):
-        return pl.ds(pl.multiple_of((2 + y) * part, part), part)
+        return pltpu.make_async_copy(w_v.at[band(5, lanes)], wgrad_hbm.at[:, lanes], sem_res.at[q])
+
+    def came(c, carry):
+        g_copy(c).wait_recv()
+        return carry
+
+    lax.fori_loop(0, chunks, came, 0)
+    nrow_copy().wait_recv()
+    pl.semaphore_wait(ready, 5)
+
+    def high_product(whose, lanes, high):
+        mine = nt_v[:, pl.ds(pl.multiple_of(row * 2 * part + whose * part, part), part)].reshape(share, local)
+        theirs = nrow_v[:, pl.ds(pl.multiple_of(whose * part, part), part)].reshape(share, local)
+        return (
+            jnp.dot(mine, gown_v[:, lanes], preferred_element_type=f32)
+            + jnp.dot(theirs, gy_v[:, high], preferred_element_type=f32)
+        ).astype(bf16)
+
+    def product2(q, carry):
+        @pl.when(q < 12)
+        def _():
+            lanes = lanes_of(q)
+            high = pl.ds(pl.multiple_of((q - Z_UNITS) * unit, unit), unit)
+            w_v[band(6, lanes, 4)] = high_product(1 - core, lanes, high)
+            core_copy2(q).start()
+            w_v[band(10, lanes, 4)] = high_product(core, lanes, high)
+
+        @pl.when(q > Z_UNITS)
+        def _():
+            lanes = lanes_of(q - 1)
+            core_copy2(q - 1).wait_recv()
+            w_v[band(10, lanes, 4)] = (
+                w_v[band(10, lanes, 4)].astype(f32) + wt_v[band(3, lanes, 4)].astype(f32)
+            ).astype(bf16)
+            for slot in range(3):
+                z_copy2(q - 1, slot).start()
+
+        return carry
+
+    lax.fori_loop(Z_UNITS, 13, product2, 0)
+
+    def arrived(c, carry):
+        for slot in range(3):
+            z_copy(c, slot).wait_recv()
+        return carry
+
+    for slot in range(3):
+        ncopy(slot).wait_recv()
+    lax.fori_loop(0, chunks, arrived, 0)
+
+    def low_product(y, whose, lanes):
+        lines = pl.ds(pl.multiple_of(y * 2 * part + whose * part, part), part)
+        return (
+            jnp.dot(ngat_v[lines, pl.ds(0, local)], gown_v[:, lanes], preferred_element_type=f32)
+            + jnp.dot(ngat_v[lines, pl.ds(local, 3 * local)], gz_v[:, lanes], preferred_element_type=f32)
+        ).astype(bf16)
+
+    def one_of(first, which):
+        return pl.ds(pl.multiple_of((first + which) * part, part), part)
 
     def product(q, carry):
-        @pl.when(q < GRAD_PIECES)
+        @pl.when(q < Z_UNITS)
         def _():
             lanes = lanes_of(q)
             for y in range(2):
-                w_v[held(y), lanes] = jnp.dot(
-                    ngat_v[band(y, 1 - core), :], ggat_v[:, lanes], preferred_element_type=f32).astype(bf16)
+                w_v[band(y, lanes)] = low_product(y, 1 - core, lanes)
                 core_copy(q, y).start()
             for y in range(2):
-                w_v[held(2 + y), lanes] = jnp.dot(
-                    ngat_v[band(y, core), :], ggat_v[:, lanes], preferred_element_type=f32).astype(bf16)
+                w_v[band(2 + y, lanes)] = low_product(y, core, lanes)
 
         @pl.when(q >= 1)
         def _():
             lanes = lanes_of(q - 1)
             for y in range(2):
                 core_copy(q - 1, y).wait_recv()
-            w_v[held(4), lanes] = (
-                w_v[own_rows(1 - row), lanes].astype(f32) + crecv_v[1 - row, :, lanes].astype(f32)
+            w_v[band(4, lanes)] = (
+                w_v[one_of(2, 1 - row), lanes].astype(f32) + wt_v[one_of(0, 1 - row), lanes].astype(f32)
             ).astype(bf16)
             row_copy(q - 1).start()
 
         return carry
 
-    lax.fori_loop(0, GRAD_PIECES + 1, product, 0)
+    lax.fori_loop(0, Z_UNITS + 1, product, 0)
+
+    def total2(q, carry):
+        lanes = lanes_of(q)
+        result = w_v[sum_rows(z), lanes].astype(f32)
+        for slot in range(3):
+            z_copy2(q, slot).wait_recv()
+            result += wt_v[band(7 + slot, lanes)].astype(f32)
+        w_v[band(5, lanes)] = result.astype(bf16)
+        res_copy(q).start()
+        return carry
 
     def total(q, carry):
         lanes = lanes_of(q)
         row_copy(q).wait_recv()
-        w_v[held(5), lanes] = (
-            w_v[own_rows(row), lanes].astype(f32) + crecv_v[row, :, lanes].astype(f32)
-            + yrecv_v[:, lanes].astype(f32)
+        w_v[band(5, lanes)] = (
+            w_v[one_of(2, row), lanes].astype(f32) + wt_v[one_of(0, row), lanes].astype(f32)
+            + wt_v[band(2, lanes)].astype(f32)
         ).astype(bf16)
         res_copy(q).start()
         return carry
 
-    lax.fori_loop(0, GRAD_PIECES, total, 0)
+    lax.fori_loop(Z_UNITS, 12, total2, 0)
+    lax.fori_loop(0, Z_UNITS, total, 0)
 
     def finish(c, carry):
         out_copy(c).wait()
-        to_up(c).wait_send()
-        to_down(c).wait_send()
-        pass_up(c).wait_send()
-        pass_down(c).wait_send()
+        g_copy(c).wait_send()
+        for slot in range(3):
+            z_copy(c, slot).wait_send()
 
         @pl.when(s == 0)
         def _():
@@ -470,17 +530,25 @@
 
     lax.fori_loop(0, chunks, finish, 0)
 
-    def finish_grad(q, carry):
+    def finish_low(q, carry):
         for y in range(2):
             core_copy(q, y).wait_send()
         row_copy(q).wait_send()
         res_copy(q).wait()
         return carry
 
-    lax.fori_loop(0, GRAD_PIECES, finish_grad, 0)
-    ncopy(1, z_up, dev_up).wait_send()
-    ncopy(2, z_down, dev_down).wait_send()
-    ncopy(3, z_far, dev_far).wait_send()
+    def finish_high(q, carry):
+        core_copy2(q).wait_send()
+        for slot in range(3):
+            z_copy2(q, slot).wait_send()
+        res_copy(q).wait()
+        return carry
+
+    lax.fori_loop(0, Z_UNITS, finish_low, 0)
+    lax.fori_loop(Z_UNITS, 12, finish_high, 0)
+    for slot in range(3):
+        ncopy(slot).wait_send()
+    nrow_copy().wait_send()
 
 
 def relay(scale, inputs, sample_ids, stored, weight, norm_gain):
@@ -490,6 +558,7 @@
     chunks = local // rows
     share = width // 4
     part = share // 4
+    split = width // 12 * Z_UNITS
     any_spec = pl.BlockSpec(memory_space=pl.ANY)
     chunked = pltpu.VMEM((chunks, rows, width), bf16)
     dma = pltpu.SemaphoreType.DMA
@@ -515,20 +584,24 @@
             pltpu.VMEM((chunks, rows, 128), f32),
             pltpu.VMEM((chunks, rows, 128), f32),
             pltpu.VMEM((8, width), f32),
-            pltpu.VMEM((width, local), bf16),
+            pltpu.VMEM((4, share, local), bf16),
             pltpu.VMEM((share, 4 * local), bf16),
-            pltpu.VMEM((4 * local, width), bf16),
-            pltpu.VMEM((2, part, width), bf16),
-            pltpu.VMEM((part, width), bf16),
+            pltpu.VMEM((4, 2 * part, local), bf16),
+            pltpu.VMEM((local, width), bf16),
+            pltpu.VMEM((3 * local, split), bf16),
+            pltpu.VMEM((local, width - split), bf16),
             dma((PIECES,)), dma, dma,
             dma((chunks,)), dma((chunks,)),
             dma((chunks, PIECES)), dma((chunks, PIECES)),
             dma((chunks,)),
-            dma((3,)), dma((3,)),
-            dma((4, chunks)), dma((4, chunks)),
-            dma((GRAD_PIECES, 2)), dma((GRAD_PIECES, 2)),
-            dma((GRAD_PIECES,)), dma((GRAD_PIECES,)),
-            dma((GRAD_PIECES,)),
+            dma((4,)), dma((4,)),
+            dma((3, chunks)), dma((3, chunks)),
+            dma((chunks,)), dma((chunks,)),
+            dma((Z_UNITS, 2)), dma((Z_UNITS, 2)),
+            dma((Z_UNITS,)), dma((Z_UNITS,)),
+            dma((12,)), dma((12,)),
+            dma((3, 12)), dma((3, 12)),
+            dma((12,)), pltpu.SemaphoreType.REGULAR,
         ],
         compiler_params=pltpu.CompilerParams(
             collective_id=0, has_side_effects=True, vmem_limit_bytes=67043328),

time: 241 us -> 220 us (0.913)
  the two profiles are of different devices: /device:TPU:32 before, /device:TPU:8 now
where the time goes in v5:
time: 220 us
  Pallas kernels  215 us (98%)
  local copies, waits for them, and re-layouts  3.76 us (2%)
    pallas_call x1, Pallas kernels, relay(): pl.pallas_call(functools.partial(relay_kernel, scale), out_shape=(jax.Sha...  215 us

profile of v5, /device:TPU:8, one launch (start us, length us, event | category | flops | bytes accessed | tf_op | source)
XLA Modules:
  0.0 219.6 jit_solution(15048973395589597487)
XLA Ops:
  0.6 215.2 %relay.1 = (bf16[2,128,3072]{2,1,0:T(8,128)(2,1)}, bf16[192,3072]{1,0:T(8,128)(2,1)}) custom-call(s32[1,2]{1,0:T(1,128)} %ids_ref.1, bf16[2,128,3072]{2,1,0:T(8,128)(2,1)} %inputs_hbm.1, bf16[1,2,2,128,3072]{4,3,2,1,0:T(8,128)(2,1)} %stored_hbm.1, bf16[1,3072,3072]{2,1,0:T(8,128)(2,1)} %w_hbm.1, f32[1,3072]{1,0:T(1,128)} %gain_ref.1), custom_call_target="tpu_custom_call" | custom-call | flops 14495514624 | bytes 18874368 | tf_op jit(solution)/shard_map/relay/pallas_call | solution.py:565
  215.8 0.0 copy-start
  215.9 2.7 %copy.9 = bf16[1,2,128,3072]{3,2,1,0:T(8,128)(2,1)} copy(bf16[1,2,128,3072]{3,2,1,0:T(8,128)(2,1)} %bitcast.2) | data formatting | bytes 3145728
  218.6 0.0 copy-done
  218.6 1.0 copy.10
Async XLA Ops:
  215.8 2.8 %copy-start = (bf16[192,3072]{1,0:T(8,128)(2,1)S(1)}, bf16[192,3072]{1,0:T(8,128)(2,1)}, u32[]{:S(2)}) copy-start(bf16[192,3072]{1,0:T(8,128)(2,1)} %get-tuple-element.5) | copy-start | bytes 3538948

commit v6 on v5

--- a/solution.py
+++ b/solution.py
@@ -13,6 +13,7 @@
 CHUNK = 32
 PIECES = 4
 Z_UNITS = 7
+LAG = 2
 MESH = pl.DeviceIdType.MESH
 f32 = jnp.float32
 bf16 = jnp.bfloat16
@@ -24,7 +25,7 @@
     scale,
     ids_ref, inputs_hbm, stored_hbm, w_hbm, gain_ref,
     out_hbm, wgrad_hbm,
-    w_v, wt_v, base_v, keep_v, fin_v, clip_v, normed_v, pre_v, out_v, bin_v,
+    w_v, wt_v, base_v, keep_v, fin_v, clip_v, normed_v, pre_v, slope_v, out_v, bin_v,
     mu_v, rs_v, u_v,
     nt_v, ngat_v, nrow_v, gown_v, gz_v, gy_v,
     sem_w, sem_base, sem_keep, fsend, frecv, bsend, brecv, sem_out,
@@ -241,49 +242,60 @@
         keep(mu_v, c, n, jnp.broadcast_to(mu, (n * rows, 128)))
         keep(rs_v, c, n, jnp.broadcast_to(rs, (n * rows, 128)))
 
+        pieces = 2 * PIECES if final else PIECES
+        narrow = width // pieces
+
         def tile(j, carry2):
-            cols = cols_of(j)
+            cols = pl.ds(pl.multiple_of(j * narrow, narrow), narrow)
             if not final:
                 @pl.when(jnp.logical_and(c == 0, late))
                 def _():
                     w_copy(j).wait()
 
             v = jnp.dot(several(normed_v, c, n), w_v[:, cols], preferred_element_type=f32)
-            keep(pre_v, c, n, v, cols)
-            res = state_of(c, n, cols) + v * (0.5 + 0.5 * lax.erf(v * rsqrt2))
+            cdf = 0.5 + 0.5 * lax.erf(v * rsqrt2)
+            res = state_of(c, n, cols) + v * cdf
             keep(out_v, c, n, res.astype(bf16), cols)
             if not final:
                 kept = keep_v[sample, pl.ds(first, rows), cols].astype(f32)
                 clip_v[c, :, cols] = jnp.clip(res - kept, -delta_bound, delta_bound).astype(bf16)
                 fcopy(c, cols).start()
-            return carry2
-
-        lax.fori_loop(0, PIECES, tile, 0)
+                keep(pre_v, c, n, v, cols)
+            slope = cdf + v * (jnp.exp(-0.5 * v * v) * rsqrt2pi)
+            if not final:
+                keep(slope_v, c, n, slope.astype(bf16), cols)
+                return carry2
+            up = res * scale
+            keep(pre_v, 0, n, up, cols)
+            return push_back(c, n, cols, slope * up, v, carry2)
+
+        zero = jnp.zeros((n * rows, 1), f32)
+        sums = lax.fori_loop(0, pieces, tile, (zero, zero) if final else 0)
         for i in range(n):
             out_copy(c + i).start()
-
-    def backward(c, n, final):
+        return sums
+
+    def push_back(c, n, cols, value, v, sums):
+        gp = value.astype(bf16)
+        gown_v[chunk_rows(c, n), cols] = gp
+        wide_gp = gp.astype(f32)
+        return (
+            sums[0] + jnp.sum(wide_gp * u_v[0:1, cols], axis=-1, keepdims=True),
+            sums[1] + jnp.sum(wide_gp * v, axis=-1, keepdims=True),
+        )
+
+    def backward(c, n, sums):
+        final = sums is not None
+
         def piece(j, sums):
             cols = cols_of(j)
-            if not final:
-                bcopy(c, j).wait_recv()
-            v = several(pre_v, c, n, cols)
-            cdf = 0.5 + 0.5 * lax.erf(v * rsqrt2)
-            slope = cdf + v * (jnp.exp(-0.5 * v * v) * rsqrt2pi)
-            if final:
-                up = (state_of(c, n, cols) + v * cdf) * scale
-            else:
-                up = several(bin_v, c, n, cols).astype(f32)
-            gp = (slope * up).astype(bf16)
-            gown_v[chunk_rows(c, n), cols] = gp
-            wide_gp = gp.astype(f32)
-            return (
-                sums[0] + jnp.sum(wide_gp * u_v[0:1, cols], axis=-1, keepdims=True),
-                sums[1] + jnp.sum(wide_gp * v, axis=-1, keepdims=True),
-            )
-
-        zero = jnp.zeros((n * rows, 1), f32)
-        sums = lax.fori_loop(0, PIECES, piece, (zero, zero))
+            bcopy(c, j).wait_recv()
+            up = several(bin_v, c, n, cols).astype(f32)
+            return push_back(c, n, cols, several(slope_v, c, n, cols).astype(f32) * up, several(pre_v, c, n, cols), sums)
+
+        if not final:
+            zero = jnp.zeros((n * rows, 1), f32)
+            sums = lax.fori_loop(0, PIECES, piece, (zero, zero))
         for i in range(n):
             for slot in range(3):
                 z_copy(c + i, slot).start()
@@ -307,8 +319,7 @@
                 state = state_of(c, n, cols)
                 xhat = (state - mu) * rs
                 if final:
-                    v = several(pre_v, c, n, cols)
-                    up = (state + v * (0.5 + 0.5 * lax.erf(v * rsqrt2))) * scale
+                    up = several(pre_v, 0, n, cols)
                 else:
                     up = several(bin_v, c, n, cols).astype(f32)
                 sent = up + rs * (gn * gain_ref[:, cols] - m1 - xhat * m2)
@@ -326,14 +337,25 @@
         else:
             pl.when(has_prev)(pull)
 
-    ahead = jnp.where(s == last - 1, chunks - 2, chunks)
-
-    def step(t, carry):
-        @pl.when(t < chunks)
-        def _():
-            forward(t, 1, False)
-
-        @pl.when(jnp.logical_and(t == chunks - 1, late))
+    def forward_step(c, carry):
+        forward(c, 1, False)
+        return carry
+
+    def backward_step(c, carry):
+        backward(c, 1, None)
+        return carry
+
+    def pair_step(t, carry):
+        sums = forward(2 * t, 2, True)
+
+        backward(2 * t, 2, sums)
+        return carry
+
+    @pl.when(has_next)
+    def _():
+        lax.fori_loop(0, chunks, forward_step, 0)
+
+        @pl.when(late)
         def _():
             share_normed()
 
@@ -341,21 +363,7 @@
             def _():
                 prepare()
 
-        @pl.when(t >= ahead)
-        def _():
-            backward(t - ahead, 1, False)
-
-        return carry
-
-    def pair_step(t, carry):
-        forward(2 * t, 2, True)
-
-        backward(2 * t, 2, True)
-        return carry
-
-    @pl.when(has_next)
-    def _():
-        lax.fori_loop(0, chunks + ahead, step, 0)
+        lax.fori_loop(0, chunks, backward_step, 0)
 
     @pl.when(s == last)
     def _():
@@ -431,19 +439,19 @@
             core_copy2(q).start()
             w_v[band(10, lanes, 4)] = high_product(core, lanes, high)
 
-        @pl.when(q > Z_UNITS)
+        @pl.when(q >= Z_UNITS + LAG)
         def _():
-            lanes = lanes_of(q - 1)
-            core_copy2(q - 1).wait_recv()
+            lanes = lanes_of(q - LAG)
+            core_copy2(q - LAG).wait_recv()
             w_v[band(10, lanes, 4)] = (
                 w_v[band(10, lanes, 4)].astype(f32) + wt_v[band(3, lanes, 4)].astype(f32)
             ).astype(bf16)
             for slot in range(3):
-                z_copy2(q - 1, slot).start()
-
-        return carry
-
-    lax.fori_loop(Z_UNITS, 13, product2, 0)
+                z_copy2(q - LAG, slot).start()
+
+        return carry
+
+    lax.fori_loop(Z_UNITS, 12 + LAG, product2, 0)
 
     def arrived(c, carry):
         for slot in range(3):
@@ -474,19 +482,19 @@
             for y in range(2):
                 w_v[band(2 + y, lanes)] = low_product(y, core, lanes)
 
-        @pl.when(q >= 1)
+        @pl.when(q >= LAG)
         def _():
-            lanes = lanes_of(q - 1)
+            lanes = lanes_of(q - LAG)
             for y in range(2):
-                core_copy(q - 1, y).wait_recv()
+                core_copy(q - LAG, y).wait_recv()
             w_v[band(4, lanes)] = (
                 w_v[one_of(2, 1 - row), lanes].astype(f32) + wt_v[one_of(0, 1 - row), lanes].astype(f32)
             ).astype(bf16)
-            row_copy(q - 1).start()
-
-        return carry
-
-    lax.fori_loop(0, Z_UNITS + 1, product, 0)
+            row_copy(q - LAG).start()
+
+        return carry
+
+    lax.fori_loop(0, Z_UNITS + LAG, product, 0)
 
     def total2(q, carry):
         lanes = lanes_of(q)
@@ -580,7 +588,7 @@
             pltpu.VMEM(inputs.shape, bf16),
             chunked, chunked, chunked,
             pltpu.VMEM((chunks, rows, width), f32),
-            chunked, chunked,
+            chunked, chunked, chunked,
             pltpu.VMEM((chunks, rows, 128), f32),
             pltpu.VMEM((chunks, rows, 128), f32),
             pltpu.VMEM((8, width), f32),

time: 220 us -> 216 us (0.982)
  Pallas kernels: 215 us -> 212 us
    pallas_call x1, Pallas kernels: 215 us -> 212 us  [relay(): pl.pallas_call(functools.partial(relay_kernel, scale), out_shape=(jax.Sha...]
where the time goes in v6:
time: 216 us
  Pallas kernels  212 us (98%)
  local copies, waits for them, and re-layouts  3.76 us (2%)
    pallas_call x1, Pallas kernels, relay(): pl.pallas_call(functools.partial(relay_kernel, scale), out_shape=(jax.Sha...  212 us

profile of v6, /device:TPU:8, one launch (start us, length us, event | category | flops | bytes accessed | tf_op | source)
XLA Modules:
  0.0 216.0 jit_solution(11146925630418422380)
XLA Ops:
  0.6 211.6 %relay.1 = (bf16[2,128,3072]{2,1,0:T(8,128)(2,1)}, bf16[192,3072]{1,0:T(8,128)(2,1)}) custom-call(s32[1,2]{1,0:T(1,128)} %ids_ref.1, bf16[2,128,3072]{2,1,0:T(8,128)(2,1)} %inputs_hbm.1, bf16[1,2,2,128,3072]{4,3,2,1,0:T(8,128)(2,1)} %stored_hbm.1, bf16[1,3072,3072]{2,1,0:T(8,128)(2,1)} %w_hbm.1, f32[1,3072]{1,0:T(1,128)} %gain_ref.1), custom_call_target="tpu_custom_call" | custom-call | flops 14495514624 | bytes 18874368 | tf_op jit(solution)/shard_map/relay/pallas_call | solution.py:573
  212.3 0.0 copy-start
  212.3 2.7 %copy.9 = bf16[1,2,128,3072]{3,2,1,0:T(8,128)(2,1)} copy(bf16[1,2,128,3072]{3,2,1,0:T(8,128)(2,1)} %bitcast.2) | data formatting | bytes 3145728
  215.0 0.0 copy-done
  215.0 1.0 copy.10
Async XLA Ops:
  212.3 2.8 %copy-start = (bf16[192,3072]{1,0:T(8,128)(2,1)S(1)}, bf16[192,3072]{1,0:T(8,128)(2,1)}, u32[]{:S(2)}) copy-start(bf16[192,3072]{1,0:T(8,128)(2,1)} %get-tuple-element.5) | copy-start | bytes 3538948

commit v7 on v6

--- a/solution.py
+++ b/solution.py
@@ -13,7 +13,9 @@
 CHUNK = 32
 PIECES = 4
 Z_UNITS = 7
+VMEM_LIMIT = 64200000
 LAG = 2
+NEAR_LAG = 6
 MESH = pl.DeviceIdType.MESH
 f32 = jnp.float32
 bf16 = jnp.bfloat16
@@ -24,13 +26,13 @@
 def relay_kernel(
     scale,
     ids_ref, inputs_hbm, stored_hbm, w_hbm, gain_ref,
-    out_hbm, wgrad_hbm,
-    w_v, wt_v, base_v, keep_v, fin_v, clip_v, normed_v, pre_v, slope_v, out_v, bin_v,
+    out_v, wgrad_v,
+    w_v, wt_v, base_v, keep_v, fin_v, clip_v, normed_v, pre_v, slope_v, bin_v,
     mu_v, rs_v, u_v,
     nt_v, ngat_v, nrow_v, gown_v, gz_v, gy_v,
-    sem_w, sem_base, sem_keep, fsend, frecv, bsend, brecv, sem_out,
+    sem_w, sem_base, sem_keep, fsend, frecv, bsend, brecv,
     nsend, nrecv, zsend, zrecv, gsend, grecv, csend, crecv, ysend, yrecv,
-    csend2, crecv2, zsend2, zrecv2, sem_res, ready,
+    csend2, crecv2, zsend2, zrecv2, ready,
 ):
     s = lax.axis_index("section")
     sections = lax.axis_size("section")
@@ -170,10 +172,6 @@
     def chunk_rows(c, n=1):
         return pl.ds(pl.multiple_of(c * rows, rows), n * rows)
 
-    def out_copy(c):
-        batch, first, sample, index = place(c)
-        return pltpu.make_async_copy(out_v.at[c], out_hbm.at[batch, pl.ds(first, rows)], sem_out.at[c])
-
     circle = ((0, z_up, dev_up), (1, z_down, dev_down), (2, z_far, dev_far))
 
     def z_copy(c, slot):
@@ -255,7 +253,7 @@
             v = jnp.dot(several(normed_v, c, n), w_v[:, cols], preferred_element_type=f32)
             cdf = 0.5 + 0.5 * lax.erf(v * rsqrt2)
             res = state_of(c, n, cols) + v * cdf
-            keep(out_v, c, n, res.astype(bf16), cols)
+            out_v[batch, pl.ds(first, n * rows), cols] = res.astype(bf16)
             if not final:
                 kept = keep_v[sample, pl.ds(first, rows), cols].astype(f32)
                 clip_v[c, :, cols] = jnp.clip(res - kept, -delta_bound, delta_bound).astype(bf16)
@@ -271,8 +269,6 @@
 
         zero = jnp.zeros((n * rows, 1), f32)
         sums = lax.fori_loop(0, pieces, tile, (zero, zero) if final else 0)
-        for i in range(n):
-            out_copy(c + i).start()
         return sums
 
     def push_back(c, n, cols, value, v, sums):
@@ -405,21 +401,21 @@
     def sum_rows(z_of):
         return pl.ds(pl.multiple_of((10 + z_of) * part, part), part)
 
-    def z_copy2(q, slot):
-        lanes = lanes_of(q)
-        return remote(w_v.at[sum_rows(circle[slot][1]), lanes], wt_v.at[band(7 + slot, lanes)],
-                      zsend2.at[slot, q], zrecv2.at[slot, q], circle[slot][2])
-
-    def res_copy(q):
-        lanes = lanes_of(q)
-        return pltpu.make_async_copy(w_v.at[band(5, lanes)], wgrad_hbm.at[:, lanes], sem_res.at[q])
+    def far_half(q, side):
+        lanes = lanes_of(q)
+        lines = pl.ds(pl.multiple_of((10 + z_far) * part + side * (part // 2), part // 2), part // 2)
+        return remote(w_v.at[lines, lanes], wt_v.at[pl.ds(7 * part + side * (part // 2), part // 2), lanes],
+                      zsend2.at[side, q], zrecv2.at[side, q], circle[side][2])
+
+    def near_block(q, side):
+        lanes = lanes_of(q)
+        return remote(w_v.at[sum_rows(circle[side][1]), lanes], wt_v.at[band(8 + side, lanes)],
+                      zsend2.at[2 + side, q], zrecv2.at[2 + side, q], circle[side][2])
 
     def came(c, carry):
         g_copy(c).wait_recv()
         return carry
 
-    lax.fori_loop(0, chunks, came, 0)
-    nrow_copy().wait_recv()
     pl.semaphore_wait(ready, 5)
 
     def high_product(whose, lanes, high):
@@ -430,37 +426,37 @@
             + jnp.dot(theirs, gy_v[:, high], preferred_element_type=f32)
         ).astype(bf16)
 
-    def product2(q, carry):
-        @pl.when(q < 12)
-        def _():
-            lanes = lanes_of(q)
-            high = pl.ds(pl.multiple_of((q - Z_UNITS) * unit, unit), unit)
-            w_v[band(6, lanes, 4)] = high_product(1 - core, lanes, high)
-            core_copy2(q).start()
-            w_v[band(10, lanes, 4)] = high_product(core, lanes, high)
-
-        @pl.when(q >= Z_UNITS + LAG)
-        def _():
-            lanes = lanes_of(q - LAG)
-            core_copy2(q - LAG).wait_recv()
-            w_v[band(10, lanes, 4)] = (
-                w_v[band(10, lanes, 4)].astype(f32) + wt_v[band(3, lanes, 4)].astype(f32)
+    def product2(q):
+        lanes = lanes_of(q)
+        high = pl.ds(pl.multiple_of((q - Z_UNITS) * unit, unit), unit)
+        w_v[band(6, lanes, 4)] = high_product(1 - core, lanes, high)
+        core_copy2(q).start()
+        w_v[band(10, lanes, 4)] = high_product(core, lanes, high)
+
+    def pair_sum2(q):
+        lanes = lanes_of(q)
+        core_copy2(q).wait_recv()
+        w_v[band(10, lanes, 4)] = (
+            w_v[band(10, lanes, 4)].astype(f32) + wt_v[band(3, lanes, 4)].astype(f32)
+        ).astype(bf16)
+        for side in range(2):
+            far_half(q, side).start()
+
+    def near_sum2(q):
+        lanes = lanes_of(q)
+        for side in range(2):
+            far_half(q, side).wait_recv()
+            lines = pl.ds(pl.multiple_of((10 + circle[side][1]) * part + side * (part // 2), part // 2), part // 2)
+            w_v[lines, lanes] = (
+                w_v[lines, lanes].astype(f32)
+                + wt_v[pl.ds(7 * part + side * (part // 2), part // 2), lanes].astype(f32)
             ).astype(bf16)
-            for slot in range(3):
-                z_copy2(q - LAG, slot).start()
-
-        return carry
-
-    lax.fori_loop(Z_UNITS, 12 + LAG, product2, 0)
+            near_block(q, side).start()
 
     def arrived(c, carry):
         for slot in range(3):
             z_copy(c, slot).wait_recv()
         return carry
-
-    for slot in range(3):
-        ncopy(slot).wait_recv()
-    lax.fori_loop(0, chunks, arrived, 0)
 
     def low_product(y, whose, lanes):
         lines = pl.ds(pl.multiple_of(y * 2 * part + whose * part, part), part)
@@ -472,55 +468,89 @@
     def one_of(first, which):
         return pl.ds(pl.multiple_of((first + which) * part, part), part)
 
-    def product(q, carry):
-        @pl.when(q < Z_UNITS)
+    def product(q):
+        lanes = lanes_of(q)
+        for y in range(2):
+            w_v[band(y, lanes)] = low_product(y, 1 - core, lanes)
+            core_copy(q, y).start()
+        for y in range(2):
+            w_v[band(2 + y, lanes)] = low_product(y, core, lanes)
+
+    def pair_sum(q):
+        lanes = lanes_of(q)
+        for y in range(2):
+            core_copy(q, y).wait_recv()
+        w_v[band(4, lanes)] = (
+            w_v[one_of(2, 1 - row), lanes].astype(f32) + wt_v[one_of(0, 1 - row), lanes].astype(f32)
+        ).astype(bf16)
+        row_copy(q).start()
+
+    high_units = 12 - Z_UNITS
+    high_first = jnp.where(s == 0, 0, Z_UNITS)
+    low_first = jnp.where(s == 0, high_units, 0)
+    near_lag = jnp.where(s == 0, NEAR_LAG, 2)
+
+    def tail(t, carry):
+        def at(begin, count, work, shift):
+            @pl.when(jnp.logical_and(t >= begin, t < begin + count))
+            def _():
+                work(t - begin + shift)
+
+        @pl.when(t == high_first)
         def _():
-            lanes = lanes_of(q)
-            for y in range(2):
-                w_v[band(y, lanes)] = low_product(y, 1 - core, lanes)
-                core_copy(q, y).start()
-            for y in range(2):
-                w_v[band(2 + y, lanes)] = low_product(y, core, lanes)
-
-        @pl.when(q >= LAG)
+            nrow_copy().wait_recv()
+            lax.fori_loop(0, chunks, came, 0)
+
+        at(high_first, high_units, product2, Z_UNITS)
+        at(high_first + LAG, high_units, pair_sum2, Z_UNITS)
+
+        @pl.when(t == low_first)
         def _():
-            lanes = lanes_of(q - LAG)
-            for y in range(2):
-                core_copy(q - LAG, y).wait_recv()
-            w_v[band(4, lanes)] = (
-                w_v[one_of(2, 1 - row), lanes].astype(f32) + wt_v[one_of(0, 1 - row), lanes].astype(f32)
-            ).astype(bf16)
-            row_copy(q - LAG).start()
-
-        return carry
-
-    lax.fori_loop(0, Z_UNITS + LAG, product, 0)
+            for slot in range(3):
+                ncopy(slot).wait_recv()
+            lax.fori_loop(0, chunks, arrived, 0)
+
+        at(low_first, Z_UNITS, product, 0)
+        at(low_first + LAG, Z_UNITS, pair_sum, 0)
+        at(high_first + LAG + near_lag, high_units, near_sum2, Z_UNITS)
+        return carry
+
+    lax.fori_loop(0, jnp.where(s == 0, max(12 + LAG, LAG + NEAR_LAG + high_units), 12 + LAG + 2), tail, 0)
 
     def total2(q, carry):
         lanes = lanes_of(q)
         result = w_v[sum_rows(z), lanes].astype(f32)
-        for slot in range(3):
-            z_copy2(q, slot).wait_recv()
-            result += wt_v[band(7 + slot, lanes)].astype(f32)
-        w_v[band(5, lanes)] = result.astype(bf16)
-        res_copy(q).start()
+        for side in range(2):
+            near_block(q, side).wait_recv()
+            result += wt_v[band(8 + side, lanes)].astype(f32)
+        wgrad_v[:, lanes] = result.astype(bf16)
         return carry
 
     def total(q, carry):
         lanes = lanes_of(q)
         row_copy(q).wait_recv()
-        w_v[band(5, lanes)] = (
+        wgrad_v[:, lanes] = (
             w_v[one_of(2, row), lanes].astype(f32) + wt_v[one_of(0, row), lanes].astype(f32)
             + wt_v[band(2, lanes)].astype(f32)
         ).astype(bf16)
-        res_copy(q).start()
-        return carry
-
-    lax.fori_loop(Z_UNITS, 12, total2, 0)
-    lax.fori_loop(0, Z_UNITS, total, 0)
+        return carry
+
+    def totals(t, carry):
+        q = (t + jnp.where(s == 0, Z_UNITS, 0)) % 12
+
+        @pl.when(q < Z_UNITS)
+        def _():
+            total(q, 0)
+
+        @pl.when(q >= Z_UNITS)
+        def _():
+            total2(q, 0)
+
+        return carry
+
+    lax.fori_loop(0, 12, totals, 0)
 
     def finish(c, carry):
-        out_copy(c).wait()
         g_copy(c).wait_send()
         for slot in range(3):
             z_copy(c, slot).wait_send()
@@ -542,14 +572,13 @@
         for y in range(2):
             core_copy(q, y).wait_send()
         row_copy(q).wait_send()
-        res_copy(q).wait()
         return carry
 
     def finish_high(q, carry):
         core_copy2(q).wait_send()
-        for slot in range(3):
-            z_copy2(q, slot).wait_send()
-        res_copy(q).wait()
+        for side in range(2):
+            far_half(q, side).wait_send()
+            near_block(q, side).wait_send()
         return carry
 
     lax.fori_loop(0, Z_UNITS, finish_low, 0)
@@ -573,14 +602,14 @@
     return pl.pallas_call(
         functools.partial(relay_kernel, scale),
         out_shape=(
-            jax.ShapeDtypeStruct(inputs.shape, bf16),
-            jax.ShapeDtypeStruct((part, width), bf16),
+            pltpu.VMEM(inputs.shape, bf16),
+            pltpu.VMEM((part, width), bf16),
         ),
         in_specs=[
             pl.BlockSpec(memory_space=pltpu.SMEM), any_spec, any_spec, any_spec,
             pl.BlockSpec(memory_space=pltpu.VMEM),
         ],
-        out_specs=(any_spec, any_spec),
+        out_specs=(pl.BlockSpec(memory_space=pltpu.VMEM), pl.BlockSpec(memory_space=pltpu.VMEM)),
         scratch_shapes=[
             pltpu.VMEM((width, width), bf16),
             pltpu.VMEM((width, width), bf16),
@@ -588,7 +617,7 @@
             pltpu.VMEM(inputs.shape, bf16),
             chunked, chunked, chunked,
             pltpu.VMEM((chunks, rows, width), f32),
-            chunked, chunked, chunked,
+            chunked, chunked,
             pltpu.VMEM((chunks, rows, 128), f32),
             pltpu.VMEM((chunks, rows, 128), f32),
             pltpu.VMEM((8, width), f32),
@@ -601,18 +630,17 @@
             dma((PIECES,)), dma, dma,
             dma((chunks,)), dma((chunks,)),
             dma((chunks, PIECES)), dma((chunks, PIECES)),
-            dma((chunks,)),
             dma((4,)), dma((4,)),
             dma((3, chunks)), dma((3, chunks)),
             dma((chunks,)), dma((chunks,)),
             dma((Z_UNITS, 2)), dma((Z_UNITS, 2)),
             dma((Z_UNITS,)), dma((Z_UNITS,)),
             dma((12,)), dma((12,)),
-            dma((3, 12)), dma((3, 12)),
-            dma((12,)), pltpu.SemaphoreType.REGULAR,
+            dma((4, 12)), dma((4, 12)),
+            pltpu.SemaphoreType.REGULAR,
         ],
         compiler_params=pltpu.CompilerParams(
-            collective_id=0, has_side_effects=True, vmem_limit_bytes=67043328),
+            collective_id=0, has_side_effects=True, vmem_limit_bytes=VMEM_LIMIT),
         cost_estimate=pl.CostEstimate(
             flops=6 * local * width * width, bytes_accessed=2 * width * width, transcendentals=0),
         name="relay",

time: 216 us -> 212 us (0.981)
  Pallas kernels: 212 us -> 209 us
where the time goes in v7:
time: 212 us
  Pallas kernels  209 us (99%)
  local copies, waits for them, and re-layouts  2.16 us (1%)
    pallas_call x1, Pallas kernels, relay(): pl.pallas_call(functools.partial(relay_kernel, scale), out_shape=(pltpu.V...  209 us

profile of v7, /device:TPU:8, one launch (start us, length us, event | category | flops | bytes accessed | tf_op | source)
XLA Modules:
  0.0 212.3 jit_solution(1177066446419764375)
XLA Ops:
  0.6 209.5 %relay.1 = (bf16[2,128,3072]{2,1,0:T(8,128)(2,1)S(1)}, bf16[192,3072]{1,0:T(8,128)(2,1)S(1)}) custom-call(s32[1,2]{1,0:T(1,128)} %ids_ref.1, bf16[2,128,3072]{2,1,0:T(8,128)(2,1)} %inputs_hbm.1, bf16[1,2,2,128,3072]{4,3,2,1,0:T(8,128)(2,1)} %stored_hbm.1, bf16[1,3072,3072]{2,1,0:T(8,128)(2,1)} %w_hbm.1, f32[1,3072]{1,0:T(1,128)} %gain_ref.1), custom_call_target="tpu_custom_call" | custom-call | flops 14495514624 | bytes 18874368 | tf_op jit(solution)/shard_map/relay/pallas_call | solution.py:602
  210.1 1.1 copy.9
  211.3 1.0 copy.10

commit v8 on v7

--- a/solution.py
+++ b/solution.py
@@ -14,6 +14,7 @@
 PIECES = 4
 Z_UNITS = 7
 VMEM_LIMIT = 64200000
+FIRST_COLUMNS = 2
 LAG = 2
 NEAR_LAG = 6
 MESH = pl.DeviceIdType.MESH
@@ -75,9 +76,9 @@
     def _():
         pltpu.make_async_copy(stored_hbm.at[0, 0], base_v, sem_base).start()
 
-    for j in range(PIECES):
+    pltpu.make_async_copy(stored_hbm.at[0, 1], keep_v, sem_keep).start()
+    for j in range(FIRST_COLUMNS):
         w_copy(j).start()
-    pltpu.make_async_copy(stored_hbm.at[0, 1], keep_v, sem_keep).start()
 
     barrier = pltpu.get_barrier_semaphore()
 
@@ -98,6 +99,8 @@
         fin_v[...] = jnp.zeros_like(fin_v)
 
     pltpu.make_async_copy(inputs_hbm, base_v, sem_base).wait()
+    for j in range(FIRST_COLUMNS, PIECES):
+        w_copy(j).start()
     def prepare():
         side = 256
         line = lax.broadcasted_iota(jnp.int32, (side, side), 0)

time: 212 us -> 209 us (0.986)
    pallas_call x1, Pallas kernels: 209 us -> 207 us  [relay(): pl.pallas_call(functools.partial(relay_kernel, scale), out_shape=(pltpu.V...]
where the time goes in v8:
time: 209 us
  Pallas kernels  207 us (99%)
  local copies, waits for them, and re-layouts  2.16 us (1%)
    pallas_call x1, Pallas kernels, relay(): pl.pallas_call(functools.partial(relay_kernel, scale), out_shape=(pltpu.V...  207 us

profile of v8, /device:TPU:8, one launch (start us, length us, event | category | flops | bytes accessed | tf_op | source)
XLA Modules:
  0.0 209.3 jit_solution(10408793088112108502)
XLA Ops:
  0.6 206.5 %relay.1 = (bf16[2,128,3072]{2,1,0:T(8,128)(2,1)S(1)}, bf16[192,3072]{1,0:T(8,128)(2,1)S(1)}) custom-call(s32[1,2]{1,0:T(1,128)} %ids_ref.1, bf16[2,128,3072]{2,1,0:T(8,128)(2,1)} %inputs_hbm.1, bf16[1,2,2,128,3072]{4,3,2,1,0:T(8,128)(2,1)} %stored_hbm.1, bf16[1,3072,3072]{2,1,0:T(8,128)(2,1)} %w_hbm.1, f32[1,3072]{1,0:T(1,128)} %gain_ref.1), custom_call_target="tpu_custom_call" | custom-call | flops 14495514624 | bytes 18874368 | tf_op jit(solution)/shard_map/relay/pallas_call | solution.py:605
  207.2 1.1 copy.9
  208.3 1.0 copy.10

commit v9 on v8

--- a/solution.py
+++ b/solution.py
@@ -12,6 +12,7 @@
 delta_bound = 2.0
 CHUNK = 32
 PIECES = 4
+FINAL_PIECES = 6
 Z_UNITS = 7
 VMEM_LIMIT = 64200000
 FIRST_COLUMNS = 2
@@ -243,7 +244,7 @@
         keep(mu_v, c, n, jnp.broadcast_to(mu, (n * rows, 128)))
         keep(rs_v, c, n, jnp.broadcast_to(rs, (n * rows, 128)))
 
-        pieces = 2 * PIECES if final else PIECES
+        pieces = FINAL_PIECES if final else PIECES
         narrow = width // pieces
 
         def tile(j, carry2):

time: 209 us -> 209 us (level)
  no operation moved by 1% of the time
where the time goes in v9:
time: 209 us
  Pallas kernels  207 us (99%)
  local copies, waits for them, and re-layouts  2.16 us (1%)
    pallas_call x1, Pallas kernels, relay(): pl.pallas_call(functools.partial(relay_kernel, scale), out_shape=(pltpu.V...  207 us

profile of v9, /device:TPU:8, one launch (start us, length us, event | category | flops | bytes accessed | tf_op | source)
XLA Modules:
  0.0 209.3 jit_solution(689499306318752136)
XLA Ops:
  0.6 206.5 %relay.1 = (bf16[2,128,3072]{2,1,0:T(8,128)(2,1)S(1)}, bf16[192,3072]{1,0:T(8,128)(2,1)S(1)}) custom-call(s32[1,2]{1,0:T(1,128)} %ids_ref.1, bf16[2,128,3072]{2,1,0:T(8,128)(2,1)} %inputs_hbm.1, bf16[1,2,2,128,3072]{4,3,2,1,0:T(8,128)(2,1)} %stored_hbm.1, bf16[1,3072,3072]{2,1,0:T(8,128)(2,1)} %w_hbm.1, f32[1,3072]{1,0:T(1,128)} %gain_ref.1), custom_call_target="tpu_custom_call" | custom-call | flops 14495514624 | bytes 18874368 | tf_op jit(solution)/shard_map/relay/pallas_call | solution.py:606
  207.2 1.1 copy.9
  208.3 1.0 copy.10
